TPU v7x, 32 devices: a whole 2x2x4 slice. The times are simulated.
32 devices in a mesh: freq: 8 (over z, y), pts: 4 (over x, core).
Axes of the slice: x: 2, y: 2, z: 4, core: 2. Of those that a mesh axis runs over, the one named last changes fastest.
Arguments:
- direct: bfloat16 [8, 512, 6144], P('freq', None, 'pts'), may hold values from -6 to 6
- onsets: int32 [8, 6144], P('freq', 'pts'), may hold values from 64 to 511
- left_bases: bfloat16 [128, 24, 24, 2, 8, 256], P('freq', 'pts'), may hold values from -0.4375 to 0.4375
- right_bases: bfloat16 [128, 24, 24, 2, 8, 256], P('freq', 'pts'), may hold values from -0.25 to 0.25
- tile_ranks: int32 [128, 24, 24], P('freq', 'pts'), may hold values from 1 to 8
Outputs:
- plus_field: float32 [8, 512, 6144], P('freq', None, 'pts')
- minus_field: float32 [8, 512, 6144], P('freq', None, 'pts')
All inputs are finite; a program needn't handle non-finite values.
Results may differ from a plain program's by a relative error of at most 0.017.
Values may be sent and summed in bfloat16 or wider, within the bound.
No kernel may reach another device: no remote copies, remote signals or barrier semaphores. Data moves between devices by JAX's collectives and lax.ppermute only.
A program may use at most 256 MiB of HBM per device.

v0:
```python
import math

import jax
import jax.numpy as jnp
from jax import lax
from jax.sharding import PartitionSpec as P

NB = 256
K = 8
F = 128
ITERS = 3
NT = 512


def band_tables(freq_total, sample_total):
    bins = lax.broadcasted_iota(jnp.int32, (freq_total, sample_total), 0) + 1
    moments = lax.broadcasted_iota(jnp.int32, (freq_total, sample_total), 1)
    phases = 2.0 * math.pi / sample_total * (bins * moments % sample_total).astype(jnp.float32)
    scaling = 1.0 / math.sqrt(sample_total)
    cosine = jnp.cos(phases) * scaling
    sine = jnp.sin(phases) * scaling
    return (jnp.stack([cosine, -sine]), jnp.stack([2.0 * cosine, -2.0 * sine]))


def contract(spec, left_part, right_part):
    return jnp.einsum(spec, left_part, right_part, preferred_element_type=jnp.float32)


def conj_apply(spec, basis_real, basis_imag, vector_real, vector_imag):
    real_part = contract(spec, basis_real, vector_real) + contract(spec, basis_imag, vector_imag)
    imag_part = contract(spec, basis_real, vector_imag) - contract(spec, basis_imag, vector_real)
    return (real_part, imag_part)


def plain_apply(spec, basis_real, basis_imag, vector_real, vector_imag):
    real_part = contract(spec, basis_real, vector_real) - contract(spec, basis_imag, vector_imag)
    imag_part = contract(spec, basis_real, vector_imag) + contract(spec, basis_imag, vector_real)
    return (real_part, imag_part)


def body(direct, onsets, left_bases, right_bases, tile_ranks):
    forward_exact, inverse_exact = band_tables(F, NT)
    forward_table = forward_exact.astype(jnp.bfloat16)
    inverse_table = inverse_exact.astype(jnp.bfloat16)
    point_here = direct.shape[0]
    cells_here = direct.shape[2]
    tile_here = cells_here // NB
    freq_here = left_bases.shape[0]
    tile_count = left_bases.shape[2]
    point_total = point_here * lax.axis_size("freq")
    group_count = lax.axis_size("pts")
    moments = lax.broadcasted_iota(jnp.int32, direct.shape, 1)
    window = (moments < onsets[:, None, :]).astype(jnp.float32)
    rank_index = lax.broadcasted_iota(jnp.int32, tile_ranks.shape + (K,), 3)
    rank_mask = (rank_index < tile_ranks[..., None]).astype(jnp.bfloat16)[..., None]

    def to_band(history):
        samples = history.astype(jnp.bfloat16)
        spectrum = jnp.einsum(
            "cft,ptn->cfpn", forward_table, samples, preferred_element_type=jnp.float32
        )
        spectrum = spectrum.reshape(2, F, point_here, tile_here, NB).astype(jnp.bfloat16)
        return lax.all_to_all(spectrum, "freq", split_axis=1, concat_axis=2, tiled=True)

    def to_time(spectrum):
        returned = lax.all_to_all(
            spectrum.astype(jnp.bfloat16), "freq", split_axis=2, concat_axis=1, tiled=True
        )
        flat = returned.reshape(2, F, point_here, cells_here)
        return (
            jnp.einsum("cft,cfpn->ptn", inverse_table, flat, preferred_element_type=jnp.float32)
            * window
        )

    moved_bases = lax.all_to_all(right_bases, "pts", split_axis=2, concat_axis=1, tiled=True)

    def forward_terms(spectrum):
        real_part, imag_part = conj_apply(
            "fijkb,fpjb->fijkp",
            moved_bases[:, :, :, 0],
            moved_bases[:, :, :, 1],
            spectrum[0],
            spectrum[1],
        )
        terms = jnp.stack([real_part, imag_part]).astype(jnp.bfloat16)
        flat = terms.reshape(2, freq_here, tile_count, tile_here, K * point_total)
        arrived = lax.all_to_all(flat, "pts", split_axis=2, concat_axis=3, tiled=True)
        return arrived.reshape(2, freq_here, tile_here, tile_count, K, point_total) * rank_mask

    def adjoint_sum(rank_terms):
        flat = rank_terms.reshape(2, freq_here, tile_here, tile_count, K * point_total)
        arrived = lax.all_to_all(flat, "pts", split_axis=3, concat_axis=2, tiled=True)
        arrived = arrived.reshape(2, freq_here, group_count, tile_here, tile_here, K, point_total)
        grouped = moved_bases.reshape(freq_here, group_count, tile_here, tile_here, 2, K, NB)
        real_part, imag_part = plain_apply(
            "fgijkb,fgijkp->gfpjb",
            grouped[:, :, :, :, 0],
            grouped[:, :, :, :, 1],
            arrived[0],
            arrived[1],
        )
        partial_value = jnp.stack([real_part, imag_part], axis=1).astype(jnp.bfloat16)
        partial_value = lax.optimization_barrier(partial_value).astype(jnp.float32)
        return jnp.sum(partial_value, axis=0)

    def forward_apply(spectrum):
        terms = forward_terms(spectrum)
        real_part, imag_part = plain_apply(
            "fijkb,fijkp->fpib", left_bases[:, :, :, 0], left_bases[:, :, :, 1], terms[0], terms[1]
        )
        return jnp.stack([real_part, imag_part])

    history = direct.astype(jnp.float32)
    plus_field = history
    minus_field = jnp.zeros_like(history)
    for iteration in range(ITERS):
        reflected = to_time(forward_apply(to_band(history)))
        minus_field = minus_field + reflected
        adjoint_spectrum = to_band(reflected)
        adjoint_real_part, adjoint_imag_part = conj_apply(
            "fijkb,fpib->fijkp",
            left_bases[:, :, :, 0],
            left_bases[:, :, :, 1],
            adjoint_spectrum[0],
            adjoint_spectrum[1],
        )
        adjoint_terms = (
            jnp.stack([adjoint_real_part, adjoint_imag_part]).astype(jnp.bfloat16) * rank_mask
        )
        history = to_time(adjoint_sum(adjoint_terms))
        plus_field = plus_field + history
    return (plus_field, minus_field)


def solution(mesh):
    return jax.shard_map(
        body,
        mesh=mesh,
        in_specs=(
            P("freq", None, "pts"),
            P("freq", "pts"),
            P("freq", "pts", None, None, None, None),
            P("freq", "pts", None, None, None, None),
            P("freq", "pts", None),
        ),
        out_specs=(P("freq", None, "pts"), P("freq", None, "pts")),
        check_vma=False,
    )
```

profile of v0, /device:TPU:0, one launch (start us, length us, event | category | flops | bytes accessed | tf_op | source)
XLA Modules:
  0.0 1257.6 jit_solution(15858424129562344300)
XLA Ops:
  13.3 17.3 %copy.325 = bf16[16,6,24,2,8,256]{5,4,3,1,0,2:T(8,128)(2,1)} copy(bf16[16,6,24,2,8,256]{5,4,3,2,1,0:T(8,128)(2,1)} %param.8) | data formatting | bytes 37748736 | tf_op args[3]
  42.2 204.2 %all-to-all-done.1 = bf16[16,6,24,2,8,256]{5,4,3,1,0,2:T(8,128)(2,1)} async-done(((bf16[16,6,24,2,8,256]{5,4,3,1,0,2:T(8,128)(2,1)}), bf16[16,6,24,2,8,256]{5,4,3,1,0,2:T(8,128)(2,1)}, u32[]{:S(2)}, u32[]{:S(2)}) %all-to-all-start.1) | async-done | bytes 18874400 | tf_op jit(solution)/shard_map/all_to_all | solution.py:75
  246.4 17.3 %copy.328 = bf16[16,4,6,6,2,8,256]{6,5,4,3,2,1,0:T(8,128)(2,1)} copy(bf16[16,4,6,6,2,8,256]{6,5,4,2,0,3,1:T(8,128)(2,1)} %bitcast.15) | data formatting | bytes 37748736 | tf_op jit(solution)/shard_map/all_to_all | solution.py:75
  291.6 10.8 fusion.44
  304.9 12.8 %fusion.43 = bf16[1,16,24,6,64]{2,4,3,1,0:T(8,128)(2,1)} fusion(f32[16,6,8,24,8]{3,2,4,1,0:T(8,128)S(1)} %copy-done.7, bf16[16,24,6,1,8,256]{5,4,3,2,1,0:T(8,128)(2,1)} %copy-done, bf16[2,16,8,1,6,256]{5,2,4,1,3,0:T(8,128)(2,1)} %bitcast.822), kind=kOutput, calls=%fused_computation.88 | convolution fusion | flops 75792384 | bytes 10715136 | tf_op jit(solution)/shard_map/fijkb,fpjb->fijkp/dot_general | solution.py:26
  326.4 14.3 %fusion.118 = (bf16[16,6,24,1,8,256]{5,4,3,2,1,0:T(8,128)(2,1)}, bf16[16,6,24,1,8,256]{5,4,3,2,1,0:T(8,128)(2,1)}) fusion(bf16[16,6,24,2,8,256]{5,4,3,2,1,0:T(8,128)(2,1)} %param.7), kind=kLoop, calls=%fused_computation.208 | loop fusion | bytes 37748736 | tf_op jit(solution)/shard_map/slice | solution.py:109
  374.5 20.9 %all-to-all-done.3 = bf16[2,16,8,6,256]{4,1,3,0,2:T(8,128)(2,1)S(1)} async-done(((bf16[2,16,8,6,256]{4,1,3,0,2:T(8,128)(2,1)}), bf16[2,16,8,6,256]{4,1,3,0,2:T(8,128)(2,1)S(1)}, u32[]{:S(2)}, u32[]{:S(2)}) %all-to-all-start.3) | async-done | bytes 786464 | tf_op jit(solution)/shard_map/all_to_all | solution.py:66
  406.8 18.5 %all-to-all-done.4 = bf16[2,128,1,6,256]{4,0,3,2,1:T(2,128)(2,1)S(1)} async-done(((bf16[2,128,1,6,256]{4,0,3,2,1:T(2,128)(2,1)}), bf16[2,128,1,6,256]{4,0,3,2,1:T(2,128)(2,1)S(1)}, u32[]{:S(2)}, u32[]{:S(2)}) %all-to-all-start.4) | async-done | bytes 786464 | tf_op jit(solution)/shard_map/all_to_all | solution.py:63
  425.8 10.6 fusion.105
  436.4 10.4 fusion.104
  458.6 12.8 %fusion.49 = bf16[1,16,6,24,64]{3,4,2,1,0:T(8,128)(2,1)} fusion(f32[16,6,8,24,8]{3,2,4,1,0:T(8,128)S(1)} %fusion.104, bf16[2,16,8,1,6,256]{5,2,4,1,3,0:T(8,128)(2,1)} %bitcast.828, bf16[16,6,24,1,8,256]{5,4,3,2,1,0:T(8,128)(2,1)} %get-tuple-element.14), kind=kOutput, calls=%fused_computation.94 | convolution fusion | flops 75792384 | bytes 10715136 | tf_op jit(solution)/shard_map/fijkb,fpib->fijkp/dot_general | solution.py:26
  479.8 17.3 %copy.548 = bf16[16,6,4,6,2,8,256]{6,5,1,3,0,2,4:T(8,128)(2,1)} copy(bf16[16,6,4,6,2,8,256]{6,5,4,1,0,3,2:T(8,128)(2,1)} %bitcast.13) | data formatting | bytes 37748736 | tf_op jit(solution)/shard_map/all_to_all | solution.py:75
  511.2 9.9 copy.350
  521.1 11.0 fusion.17
  532.1 9.6 fusion.16
  541.8 11.3 fusion.37
  553.1 10.6 fusion.38
  568.8 24.1 %all_to_all.288 = bf16[2,16,8,6,256]{4,1,3,0,2:T(8,128)(2,1)S(1)} all-to-all(bf16[2,16,8,6,256]{4,1,3,0,2:T(8,128)(2,1)S(1)} %copy.355), channel_id=1, replica_groups=mesh['freq'=8,'pts'=4] {'freq'}, dimensions={2} | all-to-all | bytes 1572864 | tf_op jit(solution)/shard_map/all_to_all | solution.py:66
  597.9 24.1 %all_to_all.289 = bf16[2,128,1,6,256]{4,0,3,2,1:T(2,128)(2,1)S(1)} all-to-all(bf16[2,128,1,6,256]{4,0,3,2,1:T(2,128)(2,1)S(1)} %copy.358), channel_id=1, replica_groups=mesh['freq'=8,'pts'=4] {'freq'}, dimensions={1} | all-to-all | bytes 1572864 | tf_op jit(solution)/shard_map/all_to_all | solution.py:63
  622.5 10.6 fusion.2
  633.1 10.4 fusion.3
  655.1 12.8 %fusion.45 = bf16[1,16,24,6,64]{2,4,3,1,0:T(8,128)(2,1)} fusion(f32[16,6,8,24,8]{3,2,4,1,0:T(8,128)S(1)} %fusion.3, bf16[16,24,6,1,8,256]{5,4,3,2,1,0:T(8,128)(2,1)} %copy-done, bf16[2,16,8,1,6,256]{5,2,4,1,3,0:T(8,128)(2,1)} %bitcast.832), kind=kOutput, calls=%fused_computation.90 | convolution fusion | flops 75792384 | bytes 10715136 | tf_op jit(solution)/shard_map/fijkb,fpjb->fijkp/dot_general | solution.py:26
  672.0 12.1 all_to_all.290
  712.5 23.9 %all_to_all.291 = bf16[2,16,8,6,256]{4,1,3,0,2:T(8,128)(2,1)S(1)} all-to-all(bf16[2,16,8,6,256]{4,1,3,0,2:T(8,128)(2,1)S(1)} %copy.366), channel_id=1, replica_groups=mesh['freq'=8,'pts'=4] {'freq'}, dimensions={2} | all-to-all | bytes 1572864 | tf_op jit(solution)/shard_map/all_to_all | solution.py:66
  741.4 23.2 %all_to_all.292 = bf16[2,128,1,6,256]{4,0,3,2,1:T(2,128)(2,1)S(1)} all-to-all(bf16[2,128,1,6,256]{4,0,3,2,1:T(2,128)(2,1)S(1)} %copy.369), channel_id=1, replica_groups=mesh['freq'=8,'pts'=4] {'freq'}, dimensions={1} | all-to-all | bytes 1572864 | tf_op jit(solution)/shard_map/all_to_all | solution.py:63
  765.0 10.6 fusion.107
  775.6 10.4 fusion.106
  797.6 12.9 %fusion.51 = bf16[1,16,6,24,64]{3,4,2,1,0:T(8,128)(2,1)} fusion(f32[16,6,8,24,8]{3,2,4,1,0:T(8,128)S(1)} %fusion.106, bf16[2,16,8,1,6,256]{5,2,4,1,3,0:T(8,128)(2,1)} %bitcast.836, bf16[16,6,24,1,8,256]{5,4,3,2,1,0:T(8,128)(2,1)} %get-tuple-element.14), kind=kOutput, calls=%fused_computation.96 | convolution fusion | flops 75792384 | bytes 10715136 | tf_op jit(solution)/shard_map/fijkb,fpib->fijkp/dot_general | solution.py:26
  814.7 11.9 all_to_all.293
  840.7 10.2 copy.376
  850.9 11.0 fusion.15
  861.9 9.6 fusion.14
  871.5 11.5 fusion.39
  883.0 10.6 fusion.40
  898.8 23.5 %all_to_all.294 = bf16[2,16,8,6,256]{4,1,3,0,2:T(8,128)(2,1)S(1)} all-to-all(bf16[2,16,8,6,256]{4,1,3,0,2:T(8,128)(2,1)S(1)} %copy.381), channel_id=1, replica_groups=mesh['freq'=8,'pts'=4] {'freq'}, dimensions={2} | all-to-all | bytes 1572864 | tf_op jit(solution)/shard_map/all_to_all | solution.py:66
  927.2 23.2 %all_to_all.295 = bf16[2,128,1,6,256]{4,0,3,2,1:T(2,128)(2,1)S(1)} all-to-all(bf16[2,128,1,6,256]{4,0,3,2,1:T(2,128)(2,1)S(1)} %copy.384), channel_id=1, replica_groups=mesh['freq'=8,'pts'=4] {'freq'}, dimensions={1} | all-to-all | bytes 1572864 | tf_op jit(solution)/shard_map/all_to_all | solution.py:63
  950.9 10.5 fusion
  961.4 10.6 fusion.1
  994.3 12.4 all_to_all.296
  1035.1 23.8 %all_to_all.297 = bf16[2,16,8,6,256]{4,1,3,0,2:T(8,128)(2,1)S(1)} all-to-all(bf16[2,16,8,6,256]{4,1,3,0,2:T(8,128)(2,1)S(1)} %copy.392), channel_id=1, replica_groups=mesh['freq'=8,'pts'=4] {'freq'}, dimensions={2} | all-to-all | bytes 1572864 | tf_op jit(solution)/shard_map/all_to_all | solution.py:66
  1068.2 23.2 %all_to_all.298 = bf16[2,128,1,6,256]{4,0,3,2,1:T(2,128)(2,1)S(1)} all-to-all(bf16[2,128,1,6,256]{4,0,3,2,1:T(2,128)(2,1)S(1)} %copy.395), channel_id=1, replica_groups=mesh['freq'=8,'pts'=4] {'freq'}, dimensions={1} | all-to-all | bytes 1572864 | tf_op jit(solution)/shard_map/all_to_all | solution.py:63
  1110.8 10.1 fusion.53
  1135.5 11.9 all_to_all.299
  1161.5 9.9 copy.402
  1171.5 11.0 fusion.13
  1192.1 11.3 fusion.41
  1203.4 10.6 fusion.42
  1226.9 18.0 %all-to-all-done.18 = bf16[2,16,8,6,256]{4,1,3,0,2:T(8,128)(2,1)} async-done(((bf16[2,16,8,6,256]{4,1,3,0,2:T(8,128)(2,1)}), bf16[2,16,8,6,256]{4,1,3,0,2:T(8,128)(2,1)}, u32[]{:S(2)}, u32[]{:S(2)}) %all-to-all-start.18) | async-done | bytes 786464 | tf_op jit(solution)/shard_map/all_to_all | solution.py:66
  (300 shorter events, 385.9 us)
Async XLA Ops:
  3.7 26.9 %copy-start.5 = (bf16[1,512,1536]{1,2,0:T(8,128)(2,1)}, bf16[1,512,1536]{1,2,0:T(8,128)(2,1)S(1)}, u32[]{:S(2)}) copy-start(bf16[1,512,1536]{1,2,0:T(8,128)(2,1)S(1)} %copy.320) | copy-start | bytes 4718596
  6.0 27.5 %all-to-all-start = ((bf16[2,128,1,6,256]{4,0,3,2,1:T(2,128)(2,1)}), bf16[2,128,1,6,256]{4,0,3,2,1:T(2,128)(2,1)S(1)}, u32[]{:S(2)}, u32[]{:S(2)}) async-start(bf16[2,128,1,6,256]{4,0,3,2,1:T(2,128)(2,1)} %copy.322), calls=%async_computation | async-start | bytes 1572864 | tf_op jit(solution)/shard_map/all_to_all | solution.py:63
  33.5 212.9 %all-to-all-start.1 = ((bf16[16,6,24,2,8,256]{5,4,3,1,0,2:T(8,128)(2,1)}), bf16[16,6,24,2,8,256]{5,4,3,1,0,2:T(8,128)(2,1)}, u32[]{:S(2)}, u32[]{:S(2)}) async-start(bf16[16,6,24,2,8,256]{5,4,3,1,0,2:T(8,128)(2,1)} %copy.325), calls=%async_computation.1 | async-start | bytes 37748736 | tf_op jit(solution)/shard_map/all_to_all | solution.py:75
  263.7 8.8 copy-start.11
  272.5 19.0 %copy-start.1 = (bf16[16,24,6,1,8,256]{5,4,3,2,1,0:T(8,128)(2,1)}, bf16[16,24,6,1,8,256]{5,4,3,2,1,0:T(8,128)(2,1)S(1)}, u32[]{:S(2)}) copy-start(bf16[16,24,6,1,8,256]{5,4,3,2,1,0:T(8,128)(2,1)S(1)} %get-tuple-element.17) | copy-start | bytes 28311556
  272.6 19.0 %copy-start = (bf16[16,24,6,1,8,256]{5,4,3,2,1,0:T(8,128)(2,1)}, bf16[16,24,6,1,8,256]{5,4,3,2,1,0:T(8,128)(2,1)S(1)}, u32[]{:S(2)}) copy-start(bf16[16,24,6,1,8,256]{5,4,3,2,1,0:T(8,128)(2,1)S(1)} %get-tuple-element.16) | copy-start | bytes 28311556
  291.6 13.3 %copy-start.7 = (f32[16,6,8,24,8]{3,2,4,1,0:T(8,128)S(1)}, f32[16,6,8,24,8]{3,2,4,1,0:T(8,128)}, u32[]{:S(2)}) copy-start(f32[16,6,8,24,8]{3,2,4,1,0:T(8,128)} %fusion.5) | copy-start | bytes 1769476
  322.5 19.0 %all-to-all-start.2 = ((bf16[4,2,36864]{2,1,0:T(2,128)(2,1)}), bf16[4,2,36864]{2,1,0:T(2,128)(2,1)S(1)}, u32[]{:S(2)}, u32[]{:S(2)}) async-start(bf16[4,2,36864]{2,1,0:T(2,128)(2,1)} %reshape.443), calls=%async_computation.2 | async-start | bytes 1179648 | tf_op jit(solution)/shard_map/all_to_all | solution.py:87
  326.4 14.3 %copy-start.24 = (s32[16,6,24]{2,0,1:T(8,128)S(1)}, s32[16,6,24]{2,0,1:T(8,128)}, u32[]{:S(2)}) copy-start(s32[16,6,24]{2,0,1:T(8,128)} %param.9) | copy-start | bytes 27652
  354.2 8.3 slice-start.18
  370.7 24.7 %all-to-all-start.3 = ((bf16[2,16,8,6,256]{4,1,3,0,2:T(8,128)(2,1)}), bf16[2,16,8,6,256]{4,1,3,0,2:T(8,128)(2,1)S(1)}, u32[]{:S(2)}, u32[]{:S(2)}) async-start(bf16[2,16,8,6,256]{4,1,3,0,2:T(8,128)(2,1)} %copy.339), calls=%async_computation.3 | async-start | bytes 1572864 | tf_op jit(solution)/shard_map/all_to_all | solution.py:66
  401.2 24.0 %all-to-all-start.4 = ((bf16[2,128,1,6,256]{4,0,3,2,1:T(2,128)(2,1)}), bf16[2,128,1,6,256]{4,0,3,2,1:T(2,128)(2,1)S(1)}, u32[]{:S(2)}, u32[]{:S(2)}) async-start(bf16[2,128,1,6,256]{4,0,3,2,1:T(2,128)(2,1)} %copy.342), calls=%async_computation.4 | async-start | bytes 1572864 | tf_op jit(solution)/shard_map/all_to_all | solution.py:63
  425.7 21.0 %copy-start.12 = (bf16[2,8,16,1,6,256]{5,1,4,2,3,0:T(8,128)(2,1)}, bf16[2,8,16,1,6,256]{5,1,4,2,3,0:T(8,128)(2,1)S(1)}, u32[]{:S(2)}) copy-start(bf16[2,8,16,1,6,256]{5,1,4,2,3,0:T(8,128)(2,1)S(1)} %copy.553) | copy-start | bytes 2359300
  425.7 21.0 %slice-start.3 = ((s8[9437184]{0:T(1024)(128)(4,1)}), s8[4194304]{0:T(1024)(128)(4,1)S(1)}, s32[]{:S(2)}) async-start(s8[9437184]{0:T(1024)(128)(4,1)} %bitcast.782), calls=%async_computation.22 | async-start | bytes 8388608
  425.7 21.0 %slice-start.4 = ((s8[9437184]{0:T(1024)(128)(4,1)}), s8[4194304]{0:T(1024)(128)(4,1)S(1)}, s32[]{:S(2)}) async-start(s8[9437184]{0:T(1024)(128)(4,1)} %bitcast.782), calls=%async_computation.23 | async-start | bytes 8388608
  436.4 10.4 slice-start.5
  476.3 20.8 %all-to-all-start.5 = ((bf16[4,2,36864]{2,1,0:T(2,128)(2,1)}), bf16[4,2,36864]{2,1,0:T(2,128)(2,1)S(1)}, u32[]{:S(2)}, u32[]{:S(2)}) async-start(bf16[4,2,36864]{2,1,0:T(2,128)(2,1)} %reshape.445), calls=%async_computation.5 | async-start | bytes 1179648 | tf_op jit(solution)/shard_map/all_to_all | solution.py:92
  511.2 21.0 %slice-start.36 = ((s8[4718592]{0:T(1024)(128)(4,1)}), s8[524288]{0:T(1024)(128)(4,1)S(1)}, s32[]{:S(2)}) async-start(s8[4718592]{0:T(1024)(128)(4,1)} %bitcast.805), calls=%async_computation.55 | async-start | bytes 1048576
  521.1 11.0 slice-start.37
  541.8 11.3 copy-start.3
  622.4 21.1 %copy-start.13 = (bf16[2,8,16,1,6,256]{5,1,4,2,3,0:T(8,128)(2,1)}, bf16[2,8,16,1,6,256]{5,1,4,2,3,0:T(8,128)(2,1)S(1)}, u32[]{:S(2)}) copy-start(bf16[2,8,16,1,6,256]{5,1,4,2,3,0:T(8,128)(2,1)S(1)} %copy.552) | copy-start | bytes 2359300
  622.4 21.1 %slice-start.30 = ((s8[9437184]{0:T(1024)(128)(4,1)}), s8[4194304]{0:T(1024)(128)(4,1)S(1)}, s32[]{:S(2)}) async-start(s8[9437184]{0:T(1024)(128)(4,1)} %bitcast.800), calls=%async_computation.49 | async-start | bytes 8388608
  622.5 21.1 %slice-start.31 = ((s8[9437184]{0:T(1024)(128)(4,1)}), s8[4194304]{0:T(1024)(128)(4,1)S(1)}, s32[]{:S(2)}) async-start(s8[9437184]{0:T(1024)(128)(4,1)} %bitcast.800), calls=%async_computation.50 | async-start | bytes 8388608
  633.1 10.4 slice-start.32
  765.0 21.0 %copy-start.14 = (bf16[2,8,16,1,6,256]{5,1,4,2,3,0:T(8,128)(2,1)}, bf16[2,8,16,1,6,256]{5,1,4,2,3,0:T(8,128)(2,1)S(1)}, u32[]{:S(2)}) copy-start(bf16[2,8,16,1,6,256]{5,1,4,2,3,0:T(8,128)(2,1)S(1)} %copy.551) | copy-start | bytes 2359300
  765.0 21.0 %slice-start.9 = ((s8[9437184]{0:T(1024)(128)(4,1)}), s8[4194304]{0:T(1024)(128)(4,1)S(1)}, s32[]{:S(2)}) async-start(s8[9437184]{0:T(1024)(128)(4,1)} %bitcast.786), calls=%async_computation.28 | async-start | bytes 8388608
  765.0 21.0 %slice-start.10 = ((s8[9437184]{0:T(1024)(128)(4,1)}), s8[4194304]{0:T(1024)(128)(4,1)S(1)}, s32[]{:S(2)}) async-start(s8[9437184]{0:T(1024)(128)(4,1)} %bitcast.786), calls=%async_computation.29 | async-start | bytes 8388608
  775.6 10.4 slice-start.11
  840.7 21.2 %slice-start.38 = ((s8[4718592]{0:T(1024)(128)(4,1)}), s8[524288]{0:T(1024)(128)(4,1)S(1)}, s32[]{:S(2)}) async-start(s8[4718592]{0:T(1024)(128)(4,1)} %bitcast.807), calls=%async_computation.57 | async-start | bytes 1048576
  850.9 11.0 slice-start.39
  871.5 11.5 copy-start.4
  950.9 21.1 %slice-start.33 = ((s8[9437184]{0:T(1024)(128)(4,1)}), s8[4194304]{0:T(1024)(128)(4,1)S(1)}, s32[]{:S(2)}) async-start(s8[9437184]{0:T(1024)(128)(4,1)} %bitcast.802), calls=%async_computation.52 | async-start | bytes 8388608
  950.9 21.1 %slice-start.34 = ((s8[9437184]{0:T(1024)(128)(4,1)}), s8[4194304]{0:T(1024)(128)(4,1)S(1)}, s32[]{:S(2)}) async-start(s8[9437184]{0:T(1024)(128)(4,1)} %bitcast.802), calls=%async_computation.53 | async-start | bytes 8388608
  961.4 10.6 slice-start.35
  1034.8 57.0 %slice-start.27 = ((s8[9437184]{0:T(1024)(128)(4,1)}), s8[1048576]{0:T(1024)(128)(4,1)S(1)}, s32[]{:S(2)}) async-start(s8[9437184]{0:T(1024)(128)(4,1)} %bitcast.798), calls=%async_computation.46 | async-start | bytes 2097152
  1060.9 30.9 %slice-start.28 = ((s8[9437184]{0:T(1024)(128)(4,1)}), s8[4194304]{0:T(1024)(128)(4,1)S(1)}, s32[]{:S(2)}) async-start(s8[9437184]{0:T(1024)(128)(4,1)} %bitcast.798), calls=%async_computation.47 | async-start | bytes 8388608
  1060.9 30.9 %slice-start.29 = ((s8[9437184]{0:T(1024)(128)(4,1)}), s8[4194304]{0:T(1024)(128)(4,1)S(1)}, s32[]{:S(2)}) async-start(s8[9437184]{0:T(1024)(128)(4,1)} %bitcast.798), calls=%async_computation.48 | async-start | bytes 8388608
  1091.8 9.5 copy-start.15
  1091.9 19.0 %slice-start.15 = ((s8[9437184]{0:T(1024)(128)(4,1)}), s8[4194304]{0:T(1024)(128)(4,1)S(1)}, s32[]{:S(2)}) async-start(s8[9437184]{0:T(1024)(128)(4,1)} %bitcast.790), calls=%async_computation.34 | async-start | bytes 8388608
  1091.9 18.9 %slice-start.16 = ((s8[9437184]{0:T(1024)(128)(4,1)}), s8[4194304]{0:T(1024)(128)(4,1)S(1)}, s32[]{:S(2)}) async-start(s8[9437184]{0:T(1024)(128)(4,1)} %bitcast.790), calls=%async_computation.35 | async-start | bytes 8388608
  1101.3 9.5 slice-start.17
  1110.8 10.2 copy-start.8
  1110.8 10.2 copy-start.16
  1161.5 21.0 %slice-start.40 = ((s8[4718592]{0:T(1024)(128)(4,1)}), s8[524288]{0:T(1024)(128)(4,1)S(1)}, s32[]{:S(2)}) async-start(s8[4718592]{0:T(1024)(128)(4,1)} %bitcast.809), calls=%async_computation.59 | async-start | bytes 1048576
  1171.5 11.0 slice-start.41
  1192.1 11.3 copy-start.2
  1220.3 24.6 %all-to-all-start.18 = ((bf16[2,16,8,6,256]{4,1,3,0,2:T(8,128)(2,1)}), bf16[2,16,8,6,256]{4,1,3,0,2:T(8,128)(2,1)}, u32[]{:S(2)}, u32[]{:S(2)}) async-start(bf16[2,16,8,6,256]{4,1,3,0,2:T(8,128)(2,1)} %copy.407), calls=%async_computation.18 | async-start | bytes 1572864 | tf_op jit(solution)/shard_map/all_to_all | solution.py:66
  1226.9 21.2 %copy-start.6 = (bf16[1,512,1536]{1,2,0:T(8,128)(2,1)S(1)}, bf16[1,512,1536]{1,2,0:T(8,128)(2,1)}, u32[]{:S(2)}) copy-start(bf16[1,512,1536]{1,2,0:T(8,128)(2,1)} %copy-done.5) | copy-start | bytes 4718596
  (27 other events, 136.8 us)
where the time goes:
time: 1260 us
  matrix products  440 us (35%)
  waiting for transfers between devices  264 us (21%)
  local copies, waits for them, and re-layouts  254 us (20%)
  blocking collectives  237 us (19%)
  starting transfers between devices  33.7 us (3%)
  other arithmetic  26.4 us (2%)
    dot_general x48, matrix products, contract(): jnp.einsum(spec, left_part, right_part, preferred_element_type=jnp.float32)  415 us
    all_to_all x1, waiting for transfers between devices, body(): lax.all_to_all(right_bases, 'pts', split_axis=2, concat_axis=1, tiled=True)  204 us
    all_to_all x4, blocking collectives, to_time(): lax.all_to_all(spectrum.astype(jnp.bfloat16), 'freq', split_axis=2, conca...  95.2 us
    all_to_all x4, blocking collectives, to_band(): lax.all_to_all(spectrum, 'freq', split_axis=1, concat_axis=2, tiled=True)  93.7 us
    all_to_all x2, waiting for transfers between devices, to_time(): lax.all_to_all(spectrum.astype(jnp.bfloat16), 'freq', split_axis=2, conca...  38.9 us
    unnamed x153, local copies, waits for them, and re-layouts  37 us
    all_to_all x2, local copies, waits for them, and re-layouts, body(): lax.all_to_all(right_bases, 'pts', split_axis=2, concat_axis=1, tiled=True)  34.6 us
    squeeze x3, local copies, waits for them, and re-layouts, adjoint_sum(): arrived[0]  30.1 us
  transfers between devices with their start and end apart: 7, of which 5 were waited for; matrix products, arithmetic and copies ran while one was open for 4% of the time, Pallas kernels for 0%

commit v1 on v0

v1 whole, which is shorter than its diff:
```python
import functools
import math

import jax
import jax.numpy as jnp
from jax import lax
from jax.experimental import pallas as pl
from jax.experimental.pallas import tpu as pltpu
from jax.sharding import PartitionSpec as P

ITERS = 3
LANES = 128


def band_tables(freq_total, sample_total):
    bins = lax.broadcasted_iota(jnp.int32, (freq_total, sample_total), 0) + 1
    moments = lax.broadcasted_iota(jnp.int32, (freq_total, sample_total), 1)
    phases = 2.0 * math.pi / sample_total * (bins * moments % sample_total).astype(jnp.float32)
    scaling = 1.0 / math.sqrt(sample_total)
    cosine = jnp.cos(phases) * scaling
    sine = jnp.sin(phases) * scaling
    return (jnp.stack([cosine, -sine]), jnp.stack([2.0 * cosine, -2.0 * sine]))


def coefficients(basis, field, pair):
    wide = field.astype(jnp.float32)
    half = wide.shape[0] // 2
    turned = jnp.concatenate([wide[half:], -wide[:half]], axis=0)
    both = jnp.concatenate([wide, turned], axis=0).astype(jnp.bfloat16)
    products = lax.dot_general(
        basis, both, (((1,), (1,)), ((), ())), preferred_element_type=jnp.float32
    )
    width = 2 * half
    direct = products[:, :width].reshape(-1, 2, pair, width)
    other = products[:, width:].reshape(-1, 2, pair, width)
    real_rows = direct[:, 0] + other[:, 1]
    imag_rows = direct[:, 1] - other[:, 0]
    return jnp.stack([real_rows, imag_rows], axis=1)


def spread(coeffs, mask_row):
    return (jnp.transpose(coeffs) * mask_row).astype(jnp.bfloat16)


def forward_kernel(x_ref, left_ref, right_ref, mask_ref, y_ref, scratch, *, rank):
    tile_rows, tile_columns, pair, nb = left_ref.shape[1:]
    width = x_ref.shape[2]
    per_group = x_ref.shape[3] // nb
    for column in range(tile_columns):
        group, place = divmod(column, per_group)
        field = x_ref[group, 0, :, place * nb : (place + 1) * nb]
        basis = right_ref[0, :, column].reshape(tile_rows * pair, nb)
        terms = coefficients(basis, field, rank)
        scratch[:, column * pair : (column + 1) * pair, :width] = terms.reshape(
            tile_rows, pair, width
        )
    for row in range(tile_rows):
        weights = spread(scratch[row], mask_ref[0, row : row + 1, :])[:width]
        basis = left_ref[0, row].reshape(tile_columns * pair, nb)
        value = jnp.dot(weights, basis, preferred_element_type=jnp.float32)
        y_ref[0, :, row * nb : (row + 1) * nb] = value.astype(jnp.bfloat16)


def adjoint_kernel(y_ref, left_ref, right_ref, mask_ref, z_ref, scratch, *, rank):
    tile_rows, tile_columns, pair, nb = left_ref.shape[1:]
    width = y_ref.shape[1]
    per_group = z_ref.shape[3] // nb
    used = tile_rows * pair
    for row in range(tile_rows):
        field = y_ref[0, :, row * nb : (row + 1) * nb]
        basis = left_ref[0, row].reshape(tile_columns * pair, nb)
        terms = coefficients(basis, field, rank)
        scratch[:, row * pair : (row + 1) * pair, :width] = terms.reshape(
            tile_columns, pair, width
        )
    for column in range(tile_columns):
        group, place = divmod(column, per_group)
        weights = spread(scratch[column], mask_ref[0, column : column + 1, :])[:width, :used]
        basis = right_ref[0, :, column].reshape(used, nb)
        value = jnp.dot(weights, basis, preferred_element_type=jnp.float32)
        z_ref[group, 0, :, place * nb : (place + 1) * nb] = value.astype(jnp.bfloat16)


def round_up(value, step):
    return -(-value // step) * step


def body(direct, onsets, left_bases, right_bases, tile_ranks):
    point_here, sample_total, cells_here = direct.shape
    freq_here, tile_rows, tile_columns, _, rank, nb = left_bases.shape
    freq_size = lax.axis_size("freq")
    pts_size = lax.axis_size("pts")
    freq_total = freq_here * freq_size
    point_total = point_here * freq_size
    width = 2 * point_total
    pair = 2 * rank
    forward_exact, inverse_exact = band_tables(freq_total, sample_total)
    forward_table = jnp.swapaxes(forward_exact, 0, 1).reshape(2 * freq_total, sample_total)
    forward_table = forward_table.astype(jnp.bfloat16)
    inverse_table = jnp.swapaxes(inverse_exact, 0, 1).reshape(2 * freq_total, sample_total)
    inverse_table = inverse_table.T.astype(jnp.bfloat16)

    moments = lax.broadcasted_iota(jnp.int32, direct.shape, 1)
    window = moments < onsets[:, None, :]

    rank_index = lax.broadcasted_iota(jnp.int32, tile_ranks.shape + (2, rank), 4)
    mask = (rank_index < tile_ranks[..., None, None]).astype(jnp.float32)
    mask = mask.reshape(freq_here, tile_rows, tile_columns, pair)
    forward_mask = mask.reshape(freq_here, tile_rows, tile_columns * pair)
    used = tile_rows * pair
    padded = round_up(used, LANES)
    adjoint_mask = jnp.swapaxes(mask, 1, 2).reshape(freq_here, tile_columns, used)
    adjoint_mask = jnp.pad(adjoint_mask, ((0, 0), (0, 0), (0, padded - used)))

    left = left_bases.reshape(freq_here, tile_rows, tile_columns, pair, nb)
    right = right_bases.reshape(freq_here, tile_rows, tile_columns, pair, nb)

    rows = freq_here * width
    to_row = lax.broadcasted_iota(jnp.int32, (rows, rows), 0)
    from_row = lax.broadcasted_iota(jnp.int32, (rows, rows), 1)
    source = (to_row % point_total) * (2 * freq_here) + to_row // point_total
    gather_rows = (source == from_row).astype(jnp.bfloat16)
    scatter_rows = gather_rows.T

    params = pltpu.CompilerParams(
        dimension_semantics=("arbitrary",), vmem_limit_bytes=48 * 1024 * 1024
    )
    basis_spec = pl.BlockSpec((1, tile_rows, tile_columns, pair, nb), lambda f: (f, 0, 0, 0, 0))
    own_spec = pl.BlockSpec((1, width, cells_here), lambda f: (f, 0, 0))
    all_spec = pl.BlockSpec((pts_size, 1, width, cells_here), lambda f: (0, f, 0, 0))
    lane_width = round_up(width, LANES)
    forward_tiles = pl.pallas_call(
        functools.partial(forward_kernel, rank=rank),
        grid=(freq_here,),
        in_specs=[
            all_spec,
            basis_spec,
            basis_spec,
            pl.BlockSpec((1, tile_rows, tile_columns * pair), lambda f: (f, 0, 0)),
        ],
        out_specs=own_spec,
        out_shape=jax.ShapeDtypeStruct((freq_here, width, cells_here), jnp.bfloat16),
        scratch_shapes=[pltpu.VMEM((tile_rows, tile_columns * pair, lane_width), jnp.float32)],
        compiler_params=params,
        name="forward_tiles",
    )
    adjoint_tiles = pl.pallas_call(
        functools.partial(adjoint_kernel, rank=rank),
        grid=(freq_here,),
        in_specs=[
            own_spec,
            basis_spec,
            basis_spec,
            pl.BlockSpec((1, tile_columns, padded), lambda f: (f, 0, 0)),
        ],
        out_specs=all_spec,
        out_shape=jax.ShapeDtypeStruct((pts_size, freq_here, width, cells_here), jnp.bfloat16),
        scratch_shapes=[pltpu.VMEM((tile_columns, padded, lane_width), jnp.float32)],
        compiler_params=params,
        name="adjoint_tiles",
    )

    def to_band(history):
        samples = history.astype(jnp.bfloat16)
        spectrum = jnp.einsum(
            "gt,ptn->pgn", forward_table, samples, preferred_element_type=jnp.float32
        ).astype(jnp.bfloat16)
        spectrum = spectrum.reshape(point_here, freq_size, 2 * freq_here, cells_here)
        spectrum = jnp.swapaxes(spectrum, 0, 1)
        arrived = lax.all_to_all(spectrum, "freq", split_axis=0, concat_axis=0, tiled=True)
        arrived = arrived.reshape(rows, cells_here)
        ordered = jnp.dot(gather_rows, arrived, preferred_element_type=jnp.float32)
        return ordered.astype(jnp.bfloat16).reshape(freq_here, width, cells_here)

    def to_time(ordered):
        ordered = ordered.reshape(freq_size, point_here, 2 * freq_here, cells_here)
        arrived = lax.all_to_all(ordered, "freq", split_axis=0, concat_axis=0, tiled=True)
        flat = jnp.swapaxes(arrived, 0, 1).reshape(point_here, 2 * freq_total, cells_here)
        field = jnp.einsum(
            "tg,pgn->ptn", inverse_table, flat, preferred_element_type=jnp.float32
        )
        return jnp.where(window, field, 0.0)

    def forward_apply(spectrum):
        everywhere = lax.all_gather(spectrum, "pts", axis=0, tiled=False)
        value = forward_tiles(everywhere, left, right, forward_mask)
        value = jnp.dot(
            scatter_rows, value.reshape(rows, cells_here), preferred_element_type=jnp.float32
        )
        return value.astype(jnp.bfloat16)

    def adjoint_apply(spectrum):
        partial_value = adjoint_tiles(spectrum, left, right, adjoint_mask)
        arrived = lax.all_to_all(partial_value, "pts", split_axis=0, concat_axis=0, tiled=True)
        arrived = arrived.reshape(pts_size, rows, cells_here)
        value = jnp.einsum(
            "rs,gsn->rn", scatter_rows, arrived, preferred_element_type=jnp.float32
        )
        return value.astype(jnp.bfloat16)

    plus_field = direct.astype(jnp.float32)
    minus_field = jnp.zeros_like(plus_field)
    history = direct
    for _ in range(ITERS):
        reflected = to_time(forward_apply(to_band(history)))
        minus_field = minus_field + reflected
        history = to_time(adjoint_apply(to_band(reflected)))
        plus_field = plus_field + history
    return (plus_field, minus_field)


def solution(mesh):
    return jax.shard_map(
        body,
        mesh=mesh,
        in_specs=(
            P("freq", None, "pts"),
            P("freq", "pts"),
            P("freq", "pts", None, None, None, None),
            P("freq", "pts", None, None, None, None),
            P("freq", "pts", None),
        ),
        out_specs=(P("freq", None, "pts"), P("freq", None, "pts")),
        check_vma=False,
    )
```

time: 1260 us -> 698 us (0.55)
  matrix products: 440 us -> 31.8 us
  local copies, waits for them, and re-layouts: 254 us -> 24.5 us
  Pallas kernels: 0 us -> 142 us
  waiting for transfers between devices: 264 us -> 148 us
  blocking collectives: 237 us -> 310 us
  other arithmetic: 26.4 us -> 3.66 us
    dot_general x60 -> x24, matrix products: 440 us -> 31.8 us  [the longest x6 11.3 us: to_time(): jnp.einsum('tg,pgn->ptn', inverse_table, flat, preferred_element_type=jnp...]
    all_to_all x7 -> x4, waiting for transfers between devices: 264 us -> 66.8 us  [the longest x2 34.2 us: to_time(): lax.all_to_all(ordered, 'freq', split_axis=0, concat_axis=0, tiled=True)]
    pallas_call x0 -> x6, Pallas kernels: none -> 142 us  [the longest x3 71.7 us: forward_apply(): value = forward_tiles(everywhere, left, right, forward_mask)]
    all_gather x0 -> x3, waiting for transfers between devices: none -> 80.8 us  [forward_apply(): everywhere = lax.all_gather(spectrum, 'pts', axis=0, tiled=False)]
    all_to_all x12 -> x11, blocking collectives: 237 us -> 310 us  [the longest x3 118 us: adjoint_apply(): lax.all_to_all(partial_value, 'pts', split_axis=0, concat_axis=0, tiled=T...]
    squeeze x6 -> x0, local copies, waits for them, and re-layouts: 54.3 us -> none  [the longest x3 30.1 us: adjoint_sum(): arrived[0]]
    all_to_all x20 -> x0, local copies, waits for them, and re-layouts: 52.2 us -> none  [the longest x2 34.6 us: body(): lax.all_to_all(right_bases, 'pts', split_axis=2, concat_axis=1, tiled=True)]
    slice x11 -> x0, local copies, waits for them, and re-layouts: 37.9 us -> none  [the longest x1 14.3 us: forward_apply(): left_bases[:, :, :, 1]]
  transfers between devices with their start and end apart: 7 -> 7, of which waited for: 5 -> 7; matrix products, arithmetic and copies ran while one was open for 4% -> 2% of each run, Pallas kernels for 0% -> 0%
where the time goes in v1:
time: 698 us; the launch traced here: 695 us
  blocking collectives  310 us (44%)
  waiting for transfers between devices  148 us (21%)
  Pallas kernels  142 us (20%)
  matrix products  31.8 us (5%)
  local copies, waits for them, and re-layouts  24.5 us (4%)
  starting transfers between devices  21.5 us (3%)
  between operations  14.3 us (2%)
    all_to_all x3, blocking collectives, adjoint_apply(): lax.all_to_all(partial_value, 'pts', split_axis=0, concat_axis=0, tiled=T...  118 us
    all_to_all x4, blocking collectives, to_time(): lax.all_to_all(ordered, 'freq', split_axis=0, concat_axis=0, tiled=True)  98.3 us
    all_to_all x4, blocking collectives, to_band(): lax.all_to_all(spectrum, 'freq', split_axis=0, concat_axis=0, tiled=True)  93.3 us
    all_gather x3, waiting for transfers between devices, forward_apply(): everywhere = lax.all_gather(spectrum, 'pts', axis=0, tiled=False)  80.8 us
    pallas_call x3, Pallas kernels, forward_apply(): value = forward_tiles(everywhere, left, right, forward_mask)  71.7 us
    pallas_call x3, Pallas kernels, adjoint_apply(): partial_value = adjoint_tiles(spectrum, left, right, adjoint_mask)  70 us
    all_to_all x2, waiting for transfers between devices, to_time(): lax.all_to_all(ordered, 'freq', split_axis=0, concat_axis=0, tiled=True)  34.2 us
    all_to_all x2, waiting for transfers between devices, to_band(): lax.all_to_all(spectrum, 'freq', split_axis=0, concat_axis=0, tiled=True)  32.6 us
  transfers between devices with their start and end apart: 7, of which 7 were waited for; matrix products, arithmetic and copies ran while one was open for 2% of the time, Pallas kernels for 0%

profile of v1, /device:TPU:0, one launch (start us, length us, event | category | flops | bytes accessed | tf_op | source)
XLA Modules:
  0.0 695.2 jit_solution(17798708181000086344)
XLA Ops:
  7.2 1.3 multiply_convert_fusion.1
  8.9 3.0 convolution_convert_fusion.8
  11.9 7.3 %all-to-all-start = ((bf16[8,1,32,1536]{3,2,1,0:T(8,128)(2,1)}), bf16[8,1,32,1536]{3,2,1,0:T(8,128)(2,1)S(1)}, u32[]{:S(2)}, u32[]{:S(2)}) async-start(bf16[8,1,32,1536]{3,2,1,0:T(8,128)(2,1)} %bitcast.6), calls=%async_computation | async-start | bytes 1572864 | tf_op jit(solution)/shard_map/all_to_all | solution.py:170
  19.3 20.1 %all-to-all-done = bf16[8,1,32,1536]{3,2,1,0:T(8,128)(2,1)S(1)} async-done(((bf16[8,1,32,1536]{3,2,1,0:T(8,128)(2,1)}), bf16[8,1,32,1536]{3,2,1,0:T(8,128)(2,1)S(1)}, u32[]{:S(2)}, u32[]{:S(2)}) %all-to-all-start) | async-done | bytes 786464 | tf_op jit(solution)/shard_map/all_to_all | solution.py:170
  39.4 1.4 convolution_convert_fusion.17
  41.6 26.9 %all-gather.4.cloned.1.call-done.x_ref = bf16[4,16,16,1536]{3,2,1,0:T(8,128)(2,1)} async-done(((bf16[1,16,16,1536]{3,2,1,0:T(8,128)(2,1)}), bf16[4,16,16,1536]{3,2,1,0:T(8,128)(2,1)}) %all-gather.4.cloned.1.call-update) | async-done | bytes 3145744 | tf_op jit(solution)/shard_map/all_gather | solution.py:185
  68.5 1.9 copy-done
  70.4 23.9 %forward_tiles.3 = bf16[16,16,1536]{2,1,0:T(8,128)(2,1)S(1)} custom-call(bf16[4,16,16,1536]{3,2,1,0:T(8,128)(2,1)S(1)} %copy-done, bf16[16,6,24,16,256]{4,3,2,1,0:T(8,128)(2,1)} %bitcast.185, bf16[16,6,24,16,256]{4,3,2,1,0:T(8,128)(2,1)} %bitcast.191, f32[16,6,384]{2,1,0:T(8,128)S(1)} %compare_convert_fusion.mask_ref), custom_call_target="tpu_custom_call" | custom-call | tf_op jit(solution)/shard_map/forward_tiles/pallas_call | solution.py:186
  94.3 1.5 convolution_convert_fusion.16
  95.8 5.5 all-to-all-start.1
  102.5 19.4 %all-to-all-done.1 = bf16[8,1,32,1536]{3,2,1,0:T(8,128)(2,1)S(1)} async-done(((bf16[8,1,32,1536]{3,2,1,0:T(8,128)(2,1)}), bf16[8,1,32,1536]{3,2,1,0:T(8,128)(2,1)S(1)}, u32[]{:S(2)}, u32[]{:S(2)}) %all-to-all-start.1) | async-done | bytes 786464 | tf_op jit(solution)/shard_map/all_to_all | solution.py:177
  122.8 1.8 fusion.4
  124.6 2.5 convolution_convert_fusion.7
  127.1 4.2 all-to-all-start.2
  132.3 1.4 copy.47
  136.7 1.3 iota.276
  138.7 12.5 %all-to-all-done.2 = bf16[8,1,32,1536]{3,2,1,0:T(8,128)(2,1)} async-done(((bf16[8,1,32,1536]{3,2,1,0:T(8,128)(2,1)}), bf16[8,1,32,1536]{3,2,1,0:T(8,128)(2,1)}, u32[]{:S(2)}, u32[]{:S(2)}) %all-to-all-start.2) | async-done | bytes 786464 | tf_op jit(solution)/shard_map/all_to_all | solution.py:170
  151.2 1.7 convolution_convert_fusion.15
  152.9 23.3 %adjoint_tiles.3 = bf16[4,16,16,1536]{3,2,1,0:T(8,128)(2,1)S(1)} custom-call(bf16[16,16,1536]{2,1,0:T(8,128)(2,1)S(1)} %bitcast.182, bf16[16,6,24,16,256]{4,3,2,1,0:T(8,128)(2,1)} %bitcast.186, bf16[16,6,24,16,256]{4,3,2,1,0:T(8,128)(2,1)} %bitcast.192, f32[16,24,128]{2,1,0:T(8,128)S(1)} %pad_convert_fusion.mask_ref), custom_call_target="tpu_custom_call" | custom-call | tf_op jit(solution)/shard_map/adjoint_tiles/pallas_call | solution.py:193
  176.3 39.4 %all_to_all.75 = bf16[4,16,16,1536]{3,2,1,0:T(8,128)(2,1)S(1)} all-to-all(bf16[4,16,16,1536]{3,2,1,0:T(8,128)(2,1)S(1)} %adjoint_tiles.3), channel_id=1, replica_groups=mesh['freq'=8,'pts'=4] {'pts'}, dimensions={0} | all-to-all | bytes 6291456 | tf_op jit(solution)/shard_map/all_to_all | solution.py:194
  217.0 23.2 %all_to_all.76 = bf16[8,1,32,1536]{3,2,1,0:T(8,128)(2,1)S(1)} all-to-all(bf16[8,1,32,1536]{3,2,1,0:T(8,128)(2,1)S(1)} %bitcast.212), channel_id=1, replica_groups=mesh['freq'=8,'pts'=4] {'freq'}, dimensions={0} | all-to-all | bytes 1572864 | tf_op jit(solution)/shard_map/all_to_all | solution.py:177
  241.6 23.1 %all_to_all.77 = bf16[8,1,32,1536]{3,2,1,0:T(8,128)(2,1)S(1)} all-to-all(bf16[8,1,32,1536]{3,2,1,0:T(8,128)(2,1)S(1)} %bitcast.204), channel_id=1, replica_groups=mesh['freq'=8,'pts'=4] {'freq'}, dimensions={0} | all-to-all | bytes 1572864 | tf_op jit(solution)/shard_map/all_to_all | solution.py:170
  264.7 1.4 convolution_convert_fusion.14
  266.3 26.8 %all-gather.6.cloned.1.call-done.x_ref = bf16[4,16,16,1536]{3,2,1,0:T(8,128)(2,1)} async-done(((bf16[1,16,16,1536]{3,2,1,0:T(8,128)(2,1)}), bf16[4,16,16,1536]{3,2,1,0:T(8,128)(2,1)}) %all-gather.6.cloned.1.call-update) | async-done | bytes 3145744 | tf_op jit(solution)/shard_map/all_gather | solution.py:185
  293.2 1.9 copy-done.1
  295.1 23.9 %forward_tiles.4 = bf16[16,16,1536]{2,1,0:T(8,128)(2,1)S(1)} custom-call(bf16[4,16,16,1536]{3,2,1,0:T(8,128)(2,1)S(1)} %copy-done.1, bf16[16,6,24,16,256]{4,3,2,1,0:T(8,128)(2,1)} %bitcast.187, bf16[16,6,24,16,256]{4,3,2,1,0:T(8,128)(2,1)} %bitcast.193, f32[16,6,384]{2,1,0:T(8,128)S(1)} %compare_convert_fusion.mask_ref), custom_call_target="tpu_custom_call" | custom-call | tf_op jit(solution)/shard_map/forward_tiles/pallas_call | solution.py:186
  319.7 25.9 %all_to_all.78 = bf16[8,1,32,1536]{3,2,1,0:T(8,128)(2,1)S(1)} all-to-all(bf16[8,1,32,1536]{3,2,1,0:T(8,128)(2,1)S(1)} %bitcast.214), channel_id=1, replica_groups=mesh['freq'=8,'pts'=4] {'freq'}, dimensions={0} | all-to-all | bytes 1572864 | tf_op jit(solution)/shard_map/all_to_all | solution.py:177
  346.9 23.6 %all_to_all.79 = bf16[8,1,32,1536]{3,2,1,0:T(8,128)(2,1)S(1)} all-to-all(bf16[8,1,32,1536]{3,2,1,0:T(8,128)(2,1)S(1)} %bitcast.205), channel_id=1, replica_groups=mesh['freq'=8,'pts'=4] {'freq'}, dimensions={0} | all-to-all | bytes 1572864 | tf_op jit(solution)/shard_map/all_to_all | solution.py:170
  371.1 23.3 %adjoint_tiles.4 = bf16[4,16,16,1536]{3,2,1,0:T(8,128)(2,1)S(1)} custom-call(bf16[16,16,1536]{2,1,0:T(8,128)(2,1)S(1)} %bitcast.184, bf16[16,6,24,16,256]{4,3,2,1,0:T(8,128)(2,1)} %bitcast.188, bf16[16,6,24,16,256]{4,3,2,1,0:T(8,128)(2,1)} %bitcast.194, f32[16,24,128]{2,1,0:T(8,128)S(1)} %pad_convert_fusion.mask_ref), custom_call_target="tpu_custom_call" | custom-call | tf_op jit(solution)/shard_map/adjoint_tiles/pallas_call | solution.py:193
  394.4 39.4 %all_to_all.80 = bf16[4,16,16,1536]{3,2,1,0:T(8,128)(2,1)S(1)} all-to-all(bf16[4,16,16,1536]{3,2,1,0:T(8,128)(2,1)S(1)} %adjoint_tiles.4), channel_id=1, replica_groups=mesh['freq'=8,'pts'=4] {'pts'}, dimensions={0} | all-to-all | bytes 6291456 | tf_op jit(solution)/shard_map/all_to_all | solution.py:194
  435.0 23.2 %all_to_all.81 = bf16[8,1,32,1536]{3,2,1,0:T(8,128)(2,1)S(1)} all-to-all(bf16[8,1,32,1536]{3,2,1,0:T(8,128)(2,1)S(1)} %bitcast.216), channel_id=1, replica_groups=mesh['freq'=8,'pts'=4] {'freq'}, dimensions={0} | all-to-all | bytes 1572864 | tf_op jit(solution)/shard_map/all_to_all | solution.py:177
  459.5 23.1 %all_to_all.82 = bf16[8,1,32,1536]{3,2,1,0:T(8,128)(2,1)S(1)} all-to-all(bf16[8,1,32,1536]{3,2,1,0:T(8,128)(2,1)S(1)} %bitcast.206), channel_id=1, replica_groups=mesh['freq'=8,'pts'=4] {'freq'}, dimensions={0} | all-to-all | bytes 1572864 | tf_op jit(solution)/shard_map/all_to_all | solution.py:170
  482.6 1.4 convolution_convert_fusion.11
  484.0 27.1 %all-gather.8.cloned.1.call-done.x_ref = bf16[4,16,16,1536]{3,2,1,0:T(8,128)(2,1)} async-done(((bf16[1,16,16,1536]{3,2,1,0:T(8,128)(2,1)}), bf16[4,16,16,1536]{3,2,1,0:T(8,128)(2,1)}) %all-gather.8.cloned.1.call-update) | async-done | bytes 3145744 | tf_op jit(solution)/shard_map/all_gather | solution.py:185
  511.1 1.9 copy-done.2
  513.0 23.9 %forward_tiles.5 = bf16[16,16,1536]{2,1,0:T(8,128)(2,1)S(1)} custom-call(bf16[4,16,16,1536]{3,2,1,0:T(8,128)(2,1)S(1)} %copy-done.2, bf16[16,6,24,16,256]{4,3,2,1,0:T(8,128)(2,1)} %bitcast.189, bf16[16,6,24,16,256]{4,3,2,1,0:T(8,128)(2,1)} %bitcast.195, f32[16,6,384]{2,1,0:T(8,128)S(1)} %compare_convert_fusion.mask_ref), custom_call_target="tpu_custom_call" | custom-call | tf_op jit(solution)/shard_map/forward_tiles/pallas_call | solution.py:186
  537.7 26.0 %all_to_all.83 = bf16[8,1,32,1536]{3,2,1,0:T(8,128)(2,1)S(1)} all-to-all(bf16[8,1,32,1536]{3,2,1,0:T(8,128)(2,1)S(1)} %bitcast.218), channel_id=1, replica_groups=mesh['freq'=8,'pts'=4] {'freq'}, dimensions={0} | all-to-all | bytes 1572864 | tf_op jit(solution)/shard_map/all_to_all | solution.py:177
  563.6 2.3 add_add_fusion
  566.5 23.6 %all_to_all.84 = bf16[8,1,32,1536]{3,2,1,0:T(8,128)(2,1)S(1)} all-to-all(bf16[8,1,32,1536]{3,2,1,0:T(8,128)(2,1)S(1)} %bitcast.211), channel_id=1, replica_groups=mesh['freq'=8,'pts'=4] {'freq'}, dimensions={0} | all-to-all | bytes 1572864 | tf_op jit(solution)/shard_map/all_to_all | solution.py:170
  590.6 23.3 %adjoint_tiles.5 = bf16[4,16,16,1536]{3,2,1,0:T(8,128)(2,1)S(1)} custom-call(bf16[16,16,1536]{2,1,0:T(8,128)(2,1)S(1)} %bitcast.180, bf16[16,6,24,16,256]{4,3,2,1,0:T(8,128)(2,1)} %bitcast.190, bf16[16,6,24,16,256]{4,3,2,1,0:T(8,128)(2,1)} %bitcast.196, f32[16,24,128]{2,1,0:T(8,128)S(1)} %pad_convert_fusion.mask_ref), custom_call_target="tpu_custom_call" | custom-call | tf_op jit(solution)/shard_map/adjoint_tiles/pallas_call | solution.py:193
  614.0 39.4 %all_to_all.85 = bf16[4,16,16,1536]{3,2,1,0:T(8,128)(2,1)S(1)} all-to-all(bf16[4,16,16,1536]{3,2,1,0:T(8,128)(2,1)S(1)} %adjoint_tiles.5), channel_id=1, replica_groups=mesh['freq'=8,'pts'=4] {'pts'}, dimensions={0} | all-to-all | bytes 6291456 | tf_op jit(solution)/shard_map/all_to_all | solution.py:194
  653.9 1.6 convolution_convert_fusion
  655.5 4.2 all-to-all-start.14
  659.7 1.6 copy.38
  661.4 3.7 copy.58
  665.1 14.8 %all-to-all-done.14 = bf16[8,1,32,1536]{3,2,1,0:T(8,128)(2,1)} async-done(((bf16[8,1,32,1536]{3,2,1,0:T(8,128)(2,1)}), bf16[8,1,32,1536]{3,2,1,0:T(8,128)(2,1)}, u32[]{:S(2)}, u32[]{:S(2)}) %all-to-all-start.14) | async-done | bytes 786464 | tf_op jit(solution)/shard_map/all_to_all | solution.py:177
  679.9 5.2 select_add_fusion
  685.1 3.5 copy.57
  (114 shorter events, 18.1 us)
Async XLA Ops:
  8.9 31.9 %copy-start.8 = (bf16[256,512]{1,0:T(8,128)(2,1)}, bf16[256,512]{1,0:T(8,128)(2,1)S(1)}, u32[]{:S(2)}) copy-start(bf16[256,512]{1,0:T(8,128)(2,1)S(1)} %convert_element_type.184) | copy-start | bytes 786436
  8.9 31.9 %copy-start.18 = (s32[16,6,24]{2,0,1:T(8,128)S(1)}, s32[16,6,24]{2,0,1:T(8,128)}, u32[]{:S(2)}) copy-start(s32[16,6,24]{2,0,1:T(8,128)} %param.9) | copy-start | bytes 27652
  11.9 27.5 %all-to-all-start = ((bf16[8,1,32,1536]{3,2,1,0:T(8,128)(2,1)}), bf16[8,1,32,1536]{3,2,1,0:T(8,128)(2,1)S(1)}, u32[]{:S(2)}, u32[]{:S(2)}) async-start(bf16[8,1,32,1536]{3,2,1,0:T(8,128)(2,1)} %bitcast.6), calls=%async_computation | async-start | bytes 1572864 | tf_op jit(solution)/shard_map/all_to_all | solution.py:170
  19.2 49.3 %all-gather.4.cloned.1.call-start = ((), (), s32[]{:S(2)}) async-start(), calls=%async_computation.15 | async-start | bytes 3932160 | tf_op jit(solution)/shard_map/all_gather | solution.py:185
  19.3 75.0 %copy-start.27 = (pred[256]{0:T(512)(128)(4,1)}, pred[256]{0:T(512)(128)(4,1)S(1)}, u32[]{:S(2)}) copy-start(pred[256]{0:T(512)(128)(4,1)S(1)} %get-tuple-element.20) | copy-start | bytes 772
  19.3 75.0 %copy-start.31 = (pred[256]{0:T(512)(128)(4,1)}, pred[256]{0:T(512)(128)(4,1)S(1)}, u32[]{:S(2)}) copy-start(pred[256]{0:T(512)(128)(4,1)S(1)} %get-tuple-element.21) | copy-start | bytes 772
  19.3 75.0 %copy-start.19 = (s32[256]{0:T(256)}, s32[256]{0:T(256)S(1)}, u32[]{:S(2)}) copy-start(s32[256]{0:T(256)S(1)} %get-tuple-element.22) | copy-start | bytes 3076
  19.3 75.0 %copy-start.23 = (s32[256]{0:T(256)}, s32[256]{0:T(256)S(1)}, u32[]{:S(2)}) copy-start(s32[256]{0:T(256)S(1)} %get-tuple-element.23) | copy-start | bytes 3076
  68.5 1.9 copy-start
  94.2 8.2 %copy-start.35 = (s32[1,1536]{1,0:T(1,128)S(1)}, s32[1,1536]{1,0:T(1,128)}, u32[]{:S(2)}) copy-start(s32[1,1536]{1,0:T(1,128)} %param.6) | copy-start | bytes 18436
  95.8 26.1 %all-to-all-start.1 = ((bf16[8,1,32,1536]{3,2,1,0:T(8,128)(2,1)}), bf16[8,1,32,1536]{3,2,1,0:T(8,128)(2,1)S(1)}, u32[]{:S(2)}, u32[]{:S(2)}) async-start(bf16[8,1,32,1536]{3,2,1,0:T(8,128)(2,1)} %bitcast.14), calls=%async_computation.1 | async-start | bytes 1572864 | tf_op jit(solution)/shard_map/all_to_all | solution.py:177
  121.9 0.9 copy-start.17
  127.1 24.2 %all-to-all-start.2 = ((bf16[8,1,32,1536]{3,2,1,0:T(8,128)(2,1)}), bf16[8,1,32,1536]{3,2,1,0:T(8,128)(2,1)}, u32[]{:S(2)}, u32[]{:S(2)}) async-start(bf16[8,1,32,1536]{3,2,1,0:T(8,128)(2,1)} %bitcast.198), calls=%async_computation.2 | async-start | bytes 1572864 | tf_op jit(solution)/shard_map/all_to_all | solution.py:170
  131.3 161.9 %all-gather.6.cloned.1.call-start = ((), (), s32[]{:S(2)}) async-start(), calls=%async_computation.16 | async-start | bytes 3932160 | tf_op jit(solution)/shard_map/all_gather | solution.py:185
  215.7 0.7 copy-start.20
  215.7 0.7 copy-start.24
  215.7 0.7 copy-start.28
  215.7 0.7 copy-start.32
  215.7 24.6 %copy-start.12 = (bf16[256,512]{1,0:T(8,128)(2,1)S(1)}, bf16[256,512]{1,0:T(8,128)(2,1)}, u32[]{:S(2)}) copy-start(bf16[256,512]{1,0:T(8,128)(2,1)} %convert_element_type.193) | copy-start | bytes 786436
  217.0 23.9 %copy-start.9 = (bf16[256,512]{1,0:T(8,128)(2,1)S(1)}, bf16[256,512]{1,0:T(8,128)(2,1)}, u32[]{:S(2)}) copy-start(bf16[256,512]{1,0:T(8,128)(2,1)} %copy-done.8) | copy-start | bytes 786436
  240.9 25.2 %copy-start.3 = (f32[1,512,1536]{1,2,0:T(8,128)}, f32[1,512,1536]{1,2,0:T(8,128)S(1)}, u32[]{:S(2)}) copy-start(f32[1,512,1536]{1,2,0:T(8,128)S(1)} %fusion.3) | copy-start | bytes 9437188
  266.1 245.0 %all-gather.8.cloned.1.call-start = ((), (), s32[]{:S(2)}) async-start(), calls=%async_computation.17 | async-start | bytes 3932160 | tf_op jit(solution)/shard_map/all_gather | solution.py:185
  293.2 1.9 copy-start.1
  295.1 23.9 %copy-start.21 = (s32[256]{0:T(256)S(1)}, s32[256]{0:T(256)}, u32[]{:S(2)}) copy-start(s32[256]{0:T(256)} %copy-done.19) | copy-start | bytes 3076
  295.1 23.9 %copy-start.25 = (s32[256]{0:T(256)S(1)}, s32[256]{0:T(256)}, u32[]{:S(2)}) copy-start(s32[256]{0:T(256)} %copy-done.23) | copy-start | bytes 3076
  295.1 23.9 %copy-start.29 = (pred[256]{0:T(512)(128)(4,1)S(1)}, pred[256]{0:T(512)(128)(4,1)}, u32[]{:S(2)}) copy-start(pred[256]{0:T(512)(128)(4,1)} %copy-done.27) | copy-start | bytes 772
  295.1 24.0 %copy-start.33 = (pred[256]{0:T(512)(128)(4,1)S(1)}, pred[256]{0:T(512)(128)(4,1)}, u32[]{:S(2)}) copy-start(pred[256]{0:T(512)(128)(4,1)} %copy-done.31) | copy-start | bytes 772
  319.0 26.7 %copy-start.13 = (bf16[256,512]{1,0:T(8,128)(2,1)S(1)}, bf16[256,512]{1,0:T(8,128)(2,1)}, u32[]{:S(2)}) copy-start(bf16[256,512]{1,0:T(8,128)(2,1)} %convert_element_type.193) | copy-start | bytes 786436
  319.7 26.6 %copy-start.10 = (bf16[256,512]{1,0:T(8,128)(2,1)S(1)}, bf16[256,512]{1,0:T(8,128)(2,1)}, u32[]{:S(2)}) copy-start(bf16[256,512]{1,0:T(8,128)(2,1)} %copy-done.8) | copy-start | bytes 786436
  346.3 24.7 %copy-start.6 = (f32[1,512,1536]{1,2,0:T(8,128)}, f32[1,512,1536]{1,2,0:T(8,128)S(1)}, u32[]{:S(2)}) copy-start(f32[1,512,1536]{1,2,0:T(8,128)S(1)} %fusion.2) | copy-start | bytes 9437188
  458.8 25.2 %copy-start.5 = (f32[1,512,1536]{1,2,0:T(8,128)}, f32[1,512,1536]{1,2,0:T(8,128)S(1)}, u32[]{:S(2)}) copy-start(f32[1,512,1536]{1,2,0:T(8,128)S(1)} %fusion.1) | copy-start | bytes 9437188
  511.1 1.9 copy-start.2
  513.0 24.0 %copy-start.22 = (s32[256]{0:T(256)S(1)}, s32[256]{0:T(256)}, u32[]{:S(2)}) copy-start(s32[256]{0:T(256)} %copy-done.19) | copy-start | bytes 3076
  513.0 24.0 %copy-start.26 = (s32[256]{0:T(256)S(1)}, s32[256]{0:T(256)}, u32[]{:S(2)}) copy-start(s32[256]{0:T(256)} %copy-done.23) | copy-start | bytes 3076
  513.0 24.0 %copy-start.30 = (pred[256]{0:T(512)(128)(4,1)S(1)}, pred[256]{0:T(512)(128)(4,1)}, u32[]{:S(2)}) copy-start(pred[256]{0:T(512)(128)(4,1)} %copy-done.27) | copy-start | bytes 772
  513.0 24.0 %copy-start.34 = (pred[256]{0:T(512)(128)(4,1)S(1)}, pred[256]{0:T(512)(128)(4,1)}, u32[]{:S(2)}) copy-start(pred[256]{0:T(512)(128)(4,1)} %copy-done.31) | copy-start | bytes 772
  513.0 50.6 %copy-start.14 = (bf16[256,512]{1,0:T(8,128)(2,1)S(1)}, bf16[256,512]{1,0:T(8,128)(2,1)}, u32[]{:S(2)}) copy-start(bf16[256,512]{1,0:T(8,128)(2,1)} %convert_element_type.193) | copy-start | bytes 786436
  537.0 26.7 %copy-start.7 = (f32[1,512,1536]{1,2,0:T(8,128)S(1)}, f32[1,512,1536]{1,2,0:T(8,128)}, u32[]{:S(2)}) copy-start(f32[1,512,1536]{1,2,0:T(8,128)} %copy-done.6) | copy-start | bytes 9437188
  563.6 2.3 copy-start.11
  653.4 6.3 copy-start.16
  655.5 24.4 %all-to-all-start.14 = ((bf16[8,1,32,1536]{3,2,1,0:T(8,128)(2,1)}), bf16[8,1,32,1536]{3,2,1,0:T(8,128)(2,1)}, u32[]{:S(2)}, u32[]{:S(2)}) async-start(bf16[8,1,32,1536]{3,2,1,0:T(8,128)(2,1)} %bitcast.82), calls=%async_computation.14 | async-start | bytes 1572864 | tf_op jit(solution)/shard_map/all_to_all | solution.py:177
  661.4 18.5 %copy-start.4 = (f32[1,512,1536]{1,2,0:T(8,128)S(1)}, f32[1,512,1536]{1,2,0:T(8,128)}, u32[]{:S(2)}) copy-start(f32[1,512,1536]{1,2,0:T(8,128)} %copy-done.3) | copy-start | bytes 9437188
  661.4 18.5 %copy-start.15 = (bf16[256,512]{1,0:T(8,128)(2,1)S(1)}, bf16[256,512]{1,0:T(8,128)(2,1)}, u32[]{:S(2)}) copy-start(bf16[256,512]{1,0:T(8,128)(2,1)} %convert_element_type.193) | copy-start | bytes 786436
Sparse Core Ops, SparseCore 0:
  40.9 27.4 all-gather.3
  266.2 26.9 all-gather.5
  484.1 26.9 all-gather.7

commit v2 on v1

--- a/solution.py
+++ b/solution.py
@@ -9,6 +9,7 @@
 from jax.sharding import PartitionSpec as P
 
 ITERS = 3
+CHUNKS = 2
 LANES = 128
 
 
@@ -95,10 +96,15 @@
     width = 2 * point_total
     pair = 2 * rank
     forward_exact, inverse_exact = band_tables(freq_total, sample_total)
-    forward_table = jnp.swapaxes(forward_exact, 0, 1).reshape(2 * freq_total, sample_total)
-    forward_table = forward_table.astype(jnp.bfloat16)
-    inverse_table = jnp.swapaxes(inverse_exact, 0, 1).reshape(2 * freq_total, sample_total)
-    inverse_table = inverse_table.T.astype(jnp.bfloat16)
+    chunks = CHUNKS if freq_here % CHUNKS == 0 else 1
+    freq_chunk = freq_here // chunks
+
+    def chunk_rows(table, chunk):
+        rows = jnp.swapaxes(table, 0, 1).reshape(freq_size, chunks, 2 * freq_chunk, sample_total)
+        return rows[:, chunk].reshape(-1, sample_total).astype(jnp.bfloat16)
+
+    forward_tables = [chunk_rows(forward_exact, chunk) for chunk in range(chunks)]
+    inverse_tables = [chunk_rows(inverse_exact, chunk).T for chunk in range(chunks)]
 
     moments = lax.broadcasted_iota(jnp.int32, direct.shape, 1)
     window = moments < onsets[:, None, :]
@@ -115,96 +121,115 @@
     left = left_bases.reshape(freq_here, tile_rows, tile_columns, pair, nb)
     right = right_bases.reshape(freq_here, tile_rows, tile_columns, pair, nb)
 
-    rows = freq_here * width
+    rows = freq_chunk * width
     to_row = lax.broadcasted_iota(jnp.int32, (rows, rows), 0)
     from_row = lax.broadcasted_iota(jnp.int32, (rows, rows), 1)
-    source = (to_row % point_total) * (2 * freq_here) + to_row // point_total
+    source = (to_row % point_total) * (2 * freq_chunk) + to_row // point_total
     gather_rows = (source == from_row).astype(jnp.bfloat16)
     scatter_rows = gather_rows.T
+    gather_rows, scatter_rows = lax.optimization_barrier((gather_rows, scatter_rows))
 
     params = pltpu.CompilerParams(
         dimension_semantics=("arbitrary",), vmem_limit_bytes=48 * 1024 * 1024
     )
-    basis_spec = pl.BlockSpec((1, tile_rows, tile_columns, pair, nb), lambda f: (f, 0, 0, 0, 0))
     own_spec = pl.BlockSpec((1, width, cells_here), lambda f: (f, 0, 0))
     all_spec = pl.BlockSpec((pts_size, 1, width, cells_here), lambda f: (0, f, 0, 0))
+    own_shape = jax.ShapeDtypeStruct((freq_chunk, width, cells_here), jnp.bfloat16)
+    all_shape = jax.ShapeDtypeStruct((pts_size, freq_chunk, width, cells_here), jnp.bfloat16)
     lane_width = round_up(width, LANES)
-    forward_tiles = pl.pallas_call(
-        functools.partial(forward_kernel, rank=rank),
-        grid=(freq_here,),
-        in_specs=[
-            all_spec,
-            basis_spec,
-            basis_spec,
-            pl.BlockSpec((1, tile_rows, tile_columns * pair), lambda f: (f, 0, 0)),
-        ],
-        out_specs=own_spec,
-        out_shape=jax.ShapeDtypeStruct((freq_here, width, cells_here), jnp.bfloat16),
-        scratch_shapes=[pltpu.VMEM((tile_rows, tile_columns * pair, lane_width), jnp.float32)],
-        compiler_params=params,
-        name="forward_tiles",
-    )
-    adjoint_tiles = pl.pallas_call(
-        functools.partial(adjoint_kernel, rank=rank),
-        grid=(freq_here,),
-        in_specs=[
-            own_spec,
-            basis_spec,
-            basis_spec,
-            pl.BlockSpec((1, tile_columns, padded), lambda f: (f, 0, 0)),
-        ],
-        out_specs=all_spec,
-        out_shape=jax.ShapeDtypeStruct((pts_size, freq_here, width, cells_here), jnp.bfloat16),
-        scratch_shapes=[pltpu.VMEM((tile_columns, padded, lane_width), jnp.float32)],
-        compiler_params=params,
-        name="adjoint_tiles",
-    )
-
-    def to_band(history):
-        samples = history.astype(jnp.bfloat16)
+    flops = 2 * freq_chunk * tile_rows * tile_columns * pair * nb * 3 * width
+    cost = pl.CostEstimate(
+        flops=flops * 16,
+        transcendentals=0,
+        bytes_accessed=freq_chunk * tile_rows * tile_columns * pair * nb * 4,
+    )
+
+    def tiles(kernel, chunk, in_spec, out_spec, out_shape, mask_shape, scratch, name):
+        first = chunk * freq_chunk
+        basis_spec = pl.BlockSpec(
+            (1, tile_rows, tile_columns, pair, nb), lambda f: (f + first, 0, 0, 0, 0)
+        )
+        return pl.pallas_call(
+            functools.partial(kernel, rank=rank),
+            grid=(freq_chunk,),
+            in_specs=[
+                in_spec,
+                basis_spec,
+                basis_spec,
+                pl.BlockSpec((1,) + mask_shape, lambda f: (f + first, 0, 0)),
+            ],
+            out_specs=out_spec,
+            out_shape=out_shape,
+            scratch_shapes=[pltpu.VMEM(scratch, jnp.float32)],
+            compiler_params=params,
+            cost_estimate=cost,
+            name=name,
+        )
+
+    def forward_tiles(spectrum, chunk):
+        call = tiles(
+            forward_kernel, chunk, all_spec, own_spec, own_shape,
+            (tile_rows, tile_columns * pair),
+            (tile_rows, tile_columns * pair, lane_width), "forward_tiles",
+        )
+        return call(spectrum, left, right, forward_mask)
+
+    def adjoint_tiles(spectrum, chunk):
+        call = tiles(
+            adjoint_kernel, chunk, own_spec, all_spec, all_shape,
+            (tile_columns, padded), (tile_columns, padded, lane_width), "adjoint_tiles",
+        )
+        return call(spectrum, left, right, adjoint_mask)
+
+    def to_band(samples, chunk):
         spectrum = jnp.einsum(
-            "gt,ptn->pgn", forward_table, samples, preferred_element_type=jnp.float32
+            "gt,ptn->pgn", forward_tables[chunk], samples, preferred_element_type=jnp.float32
         ).astype(jnp.bfloat16)
-        spectrum = spectrum.reshape(point_here, freq_size, 2 * freq_here, cells_here)
+        spectrum = spectrum.reshape(point_here, freq_size, 2 * freq_chunk, cells_here)
         spectrum = jnp.swapaxes(spectrum, 0, 1)
         arrived = lax.all_to_all(spectrum, "freq", split_axis=0, concat_axis=0, tiled=True)
         arrived = arrived.reshape(rows, cells_here)
         ordered = jnp.dot(gather_rows, arrived, preferred_element_type=jnp.float32)
-        return ordered.astype(jnp.bfloat16).reshape(freq_here, width, cells_here)
-
-    def to_time(ordered):
-        ordered = ordered.reshape(freq_size, point_here, 2 * freq_here, cells_here)
-        arrived = lax.all_to_all(ordered, "freq", split_axis=0, concat_axis=0, tiled=True)
-        flat = jnp.swapaxes(arrived, 0, 1).reshape(point_here, 2 * freq_total, cells_here)
-        field = jnp.einsum(
-            "tg,pgn->ptn", inverse_table, flat, preferred_element_type=jnp.float32
-        )
+        return ordered.astype(jnp.bfloat16).reshape(freq_chunk, width, cells_here)
+
+    def to_time(ordered_chunks):
+        field = 0.0
+        for chunk, ordered in enumerate(ordered_chunks):
+            ordered = ordered.reshape(freq_size, point_here, 2 * freq_chunk, cells_here)
+            arrived = lax.all_to_all(ordered, "freq", split_axis=0, concat_axis=0, tiled=True)
+            flat = jnp.swapaxes(arrived, 0, 1).reshape(point_here, -1, cells_here)
+            field = field + jnp.einsum(
+                "tg,pgn->ptn", inverse_tables[chunk], flat, preferred_element_type=jnp.float32
+            )
         return jnp.where(window, field, 0.0)
 
-    def forward_apply(spectrum):
+    def forward_apply(spectrum, chunk):
         everywhere = lax.all_gather(spectrum, "pts", axis=0, tiled=False)
-        value = forward_tiles(everywhere, left, right, forward_mask)
+        value = forward_tiles(everywhere, chunk)
         value = jnp.dot(
             scatter_rows, value.reshape(rows, cells_here), preferred_element_type=jnp.float32
         )
         return value.astype(jnp.bfloat16)
 
-    def adjoint_apply(spectrum):
-        partial_value = adjoint_tiles(spectrum, left, right, adjoint_mask)
-        arrived = lax.all_to_all(partial_value, "pts", split_axis=0, concat_axis=0, tiled=True)
-        arrived = arrived.reshape(pts_size, rows, cells_here)
-        value = jnp.einsum(
-            "rs,gsn->rn", scatter_rows, arrived, preferred_element_type=jnp.float32
-        )
+    def adjoint_apply(spectrum, chunk):
+        partial_value = adjoint_tiles(spectrum, chunk)
+        value = lax.psum_scatter(partial_value, "pts", scatter_dimension=0, tiled=False)
+        value = value.reshape(rows, cells_here)
+        value = jnp.dot(scatter_rows, value, preferred_element_type=jnp.float32)
         return value.astype(jnp.bfloat16)
+
+    def turn(field, apply):
+        samples = field.astype(jnp.bfloat16)
+        spectra = [to_band(samples, chunk) for chunk in range(chunks)]
+        return to_time([apply(spectrum, chunk) for chunk, spectrum in enumerate(spectra)])
 
     plus_field = direct.astype(jnp.float32)
     minus_field = jnp.zeros_like(plus_field)
     history = direct
     for _ in range(ITERS):
-        reflected = to_time(forward_apply(to_band(history)))
+        reflected = turn(history, forward_apply)
         minus_field = minus_field + reflected
-        history = to_time(adjoint_apply(to_band(reflected)))
+        history = turn(reflected, adjoint_apply)
         plus_field = plus_field + history
     return (plus_field, minus_field)
 

time: 698 us -> 641 us (0.918)
  blocking collectives: 310 us -> 152 us
  matrix products: 31.8 us -> 84.9 us
  starting transfers between devices: 21.5 us -> 71.7 us
  waiting for transfers between devices: 148 us -> 132 us
  Pallas kernels: 142 us -> 155 us
    all_to_all x7 -> x0, blocking collectives: 217 us -> none  [the longest x3 118 us: adjoint_apply(): lax.all_to_all(partial_value, 'pts', split_axis=0, concat_axis=0, tiled=T...]
    all_gather x3 -> x6, waiting for transfers between devices: 80.8 us -> 3.35 us  [forward_apply(): everywhere = lax.all_gather(spectrum, 'pts', axis=0, tiled=False)]
    reduce_scatter x0 -> x6, waiting for transfers between devices: none -> 61 us  [adjoint_apply(): lax.psum_scatter(partial_value, 'pts', scatter_dimension=0, tiled=False)]
    all_to_all x4 -> x10, blocking collectives: 93.3 us -> 152 us  [to_band(): lax.all_to_all(spectrum, 'freq', split_axis=0, concat_axis=0, tiled=True)]
    all_to_all x2 -> x12, starting transfers between devices: 9.72 us -> 59.3 us  [to_time(): lax.all_to_all(ordered, 'freq', split_axis=0, concat_axis=0, tiled=True)]
    dot_general x15 -> x30, matrix products: 22 us -> 70.2 us  [the longest x12 41.2 us: to_time(): jnp.einsum('tg,pgn->ptn', inverse_tables[chunk], flat, preferred_element_...]
    pallas_call x6 -> x12, Pallas kernels: 142 us -> 155 us  [the longest x6 79 us: adjoint_tiles(): return call(spectrum, left, right, adjoint_mask)]
    all_to_all x2 -> x12, waiting for transfers between devices: 34.2 us -> 46.7 us  [to_time(): lax.all_to_all(ordered, 'freq', split_axis=0, concat_axis=0, tiled=True)]
  transfers between devices with their start and end apart: 7 -> 26, of which waited for: 7 -> 15; matrix products, arithmetic and copies ran while one was open for 2% -> 10% of each run, Pallas kernels for 0% -> 18%
where the time goes in v2:
time: 641 us; the launch traced here: 637 us
  Pallas kernels  155 us (24%)
  blocking collectives  152 us (24%)
  waiting for transfers between devices  132 us (21%)
  matrix products  84.9 us (13%)
  starting transfers between devices  71.7 us (11%)
  local copies, waits for them, and re-layouts  24.6 us (4%)
  between operations  14.9 us (2%)
    all_to_all x10, blocking collectives, to_band(): lax.all_to_all(spectrum, 'freq', split_axis=0, concat_axis=0, tiled=True)  152 us
    pallas_call x6, Pallas kernels, adjoint_tiles(): return call(spectrum, left, right, adjoint_mask)  79 us
    pallas_call x6, Pallas kernels, forward_tiles(): return call(spectrum, left, right, forward_mask)  75.6 us
    reduce_scatter x6, waiting for transfers between devices, adjoint_apply(): lax.psum_scatter(partial_value, 'pts', scatter_dimension=0, tiled=False)  61 us
    all_to_all x12, starting transfers between devices, to_time(): lax.all_to_all(ordered, 'freq', split_axis=0, concat_axis=0, tiled=True)  59.3 us
    all_to_all x12, waiting for transfers between devices, to_time(): lax.all_to_all(ordered, 'freq', split_axis=0, concat_axis=0, tiled=True)  46.7 us
    dot_general x12, matrix products, to_time(): jnp.einsum('tg,pgn->ptn', inverse_tables[chunk], flat, preferred_element_...  41.2 us
    unnamed x86, local copies, waits for them, and re-layouts  20.7 us
  transfers between devices with their start and end apart: 26, of which 15 were waited for; matrix products, arithmetic and copies ran while one was open for 10% of the time, Pallas kernels for 18%

profile of v2, /device:TPU:0, one launch (start us, length us, event | category | flops | bytes accessed | tf_op | source)
XLA Modules:
  0.0 636.8 jit_solution(5938990564265903645)
XLA Ops:
  10.8 7.4 %all-to-all-start.2 = ((bf16[8,1,16,1536]{3,2,1,0:T(8,128)(2,1)}), bf16[8,1,16,1536]{3,2,1,0:T(8,128)(2,1)S(1)}, u32[]{:S(2)}, u32[]{:S(2)}) async-start(bf16[8,1,16,1536]{3,2,1,0:T(8,128)(2,1)} %bitcast.25), calls=%async_computation.2 | async-start | bytes 786432 | tf_op jit(solution)/shard_map/all_to_all | solution.py:190
  18.5 11.4 %all-to-all-done.2 = bf16[8,1,16,1536]{3,2,1,0:T(8,128)(2,1)S(1)} async-done(((bf16[8,1,16,1536]{3,2,1,0:T(8,128)(2,1)}), bf16[8,1,16,1536]{3,2,1,0:T(8,128)(2,1)S(1)}, u32[]{:S(2)}, u32[]{:S(2)}) %all-to-all-start.2) | async-done | bytes 393248 | tf_op jit(solution)/shard_map/all_to_all | solution.py:190
  31.4 15.4 %all_to_all.120 = bf16[8,1,16,1536]{3,2,1,0:T(8,128)(2,1)S(1)} all-to-all(bf16[8,1,16,1536]{3,2,1,0:T(8,128)(2,1)S(1)} %bitcast.499), channel_id=1, replica_groups=mesh['freq'=8,'pts'=4] {'freq'}, dimensions={0} | all-to-all | bytes 786432 | tf_op jit(solution)/shard_map/all_to_all | solution.py:190
  51.2 12.6 %forward_tiles.7 = bf16[8,16,1536]{2,1,0:T(8,128)(2,1)S(1)} custom-call(bf16[4,8,16,1536]{3,2,1,0:T(8,128)(2,1)S(1)} %copy-done, bf16[16,6,24,16,256]{4,3,2,1,0:T(8,128)(2,1)} %bitcast.433, bf16[16,6,24,16,256]{4,3,2,1,0:T(8,128)(2,1)} %bitcast.445, f32[16,6,384]{2,1,0:T(8,128)S(1)} %compare_convert_fusion.mask_ref), custom_call_target="tpu_custom_call" | custom-call | flops 7247757312 | bytes 18874368 | tf_op jit(solution)/shard_map/forward_tiles/pallas_call | solution.py:175
  64.8 5.6 all-to-all-start.3
  73.1 12.6 %forward_tiles.6 = bf16[8,16,1536]{2,1,0:T(8,128)(2,1)S(1)} custom-call(bf16[4,8,16,1536]{3,2,1,0:T(8,128)(2,1)S(1)} %copy-done.1, bf16[16,6,24,16,256]{4,3,2,1,0:T(8,128)(2,1)} %bitcast.434, bf16[16,6,24,16,256]{4,3,2,1,0:T(8,128)(2,1)} %bitcast.446, f32[16,6,384]{2,1,0:T(8,128)S(1)} %compare_convert_fusion.mask_ref), custom_call_target="tpu_custom_call" | custom-call | flops 7247757312 | bytes 18874368 | tf_op jit(solution)/shard_map/forward_tiles/pallas_call | solution.py:175
  86.7 5.5 all-to-all-start.1
  94.9 9.5 %all-to-all-done.1 = bf16[8,1,16,1536]{3,2,1,0:T(8,128)(2,1)} async-done(((bf16[8,1,16,1536]{3,2,1,0:T(8,128)(2,1)}), bf16[8,1,16,1536]{3,2,1,0:T(8,128)(2,1)}, u32[]{:S(2)}, u32[]{:S(2)}) %all-to-all-start.1) | async-done | bytes 393248 | tf_op jit(solution)/shard_map/all_to_all | solution.py:199
  108.5 4.1 all-to-all-start.6
  115.2 8.9 %all-to-all-done.6 = bf16[8,1,16,1536]{3,2,1,0:T(8,128)(2,1)} async-done(((bf16[8,1,16,1536]{3,2,1,0:T(8,128)(2,1)}), bf16[8,1,16,1536]{3,2,1,0:T(8,128)(2,1)}, u32[]{:S(2)}, u32[]{:S(2)}) %all-to-all-start.6) | async-done | bytes 393248 | tf_op jit(solution)/shard_map/all_to_all | solution.py:190
  125.4 13.1 %adjoint_tiles.7 = bf16[4,8,16,1536]{3,2,1,0:T(8,128)(2,1)} custom-call(bf16[8,16,1536]{2,1,0:T(8,128)(2,1)S(1)} %bitcast.425, bf16[16,6,24,16,256]{4,3,2,1,0:T(8,128)(2,1)} %bitcast.435, bf16[16,6,24,16,256]{4,3,2,1,0:T(8,128)(2,1)} %bitcast.447, f32[16,24,128]{2,1,0:T(8,128)S(1)} %pad_convert_fusion.mask_ref), custom_call_target="tpu_custom_call" | custom-call | flops 7247757312 | bytes 18874368 | tf_op jit(solution)/shard_map/adjoint_tiles/pallas_call | solution.py:182
  140.2 15.3 %all_to_all.121 = bf16[8,1,16,1536]{3,2,1,0:T(8,128)(2,1)S(1)} all-to-all(bf16[8,1,16,1536]{3,2,1,0:T(8,128)(2,1)S(1)} %bitcast.500), channel_id=1, replica_groups=mesh['freq'=8,'pts'=4] {'freq'}, dimensions={0} | all-to-all | bytes 786432 | tf_op jit(solution)/shard_map/all_to_all | solution.py:190
  155.7 13.2 %adjoint_tiles.6 = bf16[4,8,16,1536]{3,2,1,0:T(8,128)(2,1)} custom-call(bf16[8,16,1536]{2,1,0:T(8,128)(2,1)S(1)} %bitcast.426, bf16[16,6,24,16,256]{4,3,2,1,0:T(8,128)(2,1)} %bitcast.436, bf16[16,6,24,16,256]{4,3,2,1,0:T(8,128)(2,1)} %bitcast.448, f32[16,24,128]{2,1,0:T(8,128)S(1)} %pad_convert_fusion.mask_ref), custom_call_target="tpu_custom_call" | custom-call | flops 7247757312 | bytes 18874368 | tf_op jit(solution)/shard_map/adjoint_tiles/pallas_call | solution.py:182
  171.0 4.1 all-to-all-start.7
  175.1 20.7 %reduce-scatter.7.cloned.1.call-done = bf16[1,8,16,1536]{3,2,1,0:T(8,128)(2,1)} async-done(((bf16[4,8,16,1536]{3,2,1,0:T(8,128)(2,1)}), bf16[1,8,16,1536]{3,2,1,0:T(8,128)(2,1)}) %reduce-scatter.7.cloned.1.call-update) | async-done | bytes 393232 | tf_op jit(solution)/shard_map/reduce_scatter | solution.py:216
  197.8 5.5 all-to-all-start.5
  206.9 8.1 %all-to-all-done.5 = bf16[8,1,16,1536]{3,2,1,0:T(8,128)(2,1)} async-done(((bf16[8,1,16,1536]{3,2,1,0:T(8,128)(2,1)}), bf16[8,1,16,1536]{3,2,1,0:T(8,128)(2,1)}, u32[]{:S(2)}, u32[]{:S(2)}) %all-to-all-start.5) | async-done | bytes 393248 | tf_op jit(solution)/shard_map/all_to_all | solution.py:199
  220.1 15.3 %all_to_all.122 = bf16[8,1,16,1536]{3,2,1,0:T(8,128)(2,1)S(1)} all-to-all(bf16[8,1,16,1536]{3,2,1,0:T(8,128)(2,1)S(1)} %bitcast.501), channel_id=1, replica_groups=mesh['freq'=8,'pts'=4] {'freq'}, dimensions={0} | all-to-all | bytes 786432 | tf_op jit(solution)/shard_map/all_to_all | solution.py:190
  239.0 14.8 %all_to_all.123 = bf16[8,1,16,1536]{3,2,1,0:T(8,128)(2,1)S(1)} all-to-all(bf16[8,1,16,1536]{3,2,1,0:T(8,128)(2,1)S(1)} %bitcast.502), channel_id=1, replica_groups=mesh['freq'=8,'pts'=4] {'freq'}, dimensions={0} | all-to-all | bytes 786432 | tf_op jit(solution)/shard_map/all_to_all | solution.py:190
  256.3 12.7 %forward_tiles.9 = bf16[8,16,1536]{2,1,0:T(8,128)(2,1)S(1)} custom-call(bf16[4,8,16,1536]{3,2,1,0:T(8,128)(2,1)S(1)} %copy-done.2, bf16[16,6,24,16,256]{4,3,2,1,0:T(8,128)(2,1)} %bitcast.437, bf16[16,6,24,16,256]{4,3,2,1,0:T(8,128)(2,1)} %bitcast.449, f32[16,6,384]{2,1,0:T(8,128)S(1)} %compare_convert_fusion.mask_ref), custom_call_target="tpu_custom_call" | custom-call | flops 7247757312 | bytes 18874368 | tf_op jit(solution)/shard_map/forward_tiles/pallas_call | solution.py:175
  270.0 4.6 all-to-all-start.11
  276.4 12.5 %forward_tiles.8 = bf16[8,16,1536]{2,1,0:T(8,128)(2,1)S(1)} custom-call(bf16[4,8,16,1536]{3,2,1,0:T(8,128)(2,1)S(1)} %copy-done.5, bf16[16,6,24,16,256]{4,3,2,1,0:T(8,128)(2,1)} %bitcast.438, bf16[16,6,24,16,256]{4,3,2,1,0:T(8,128)(2,1)} %bitcast.450, f32[16,6,384]{2,1,0:T(8,128)S(1)} %compare_convert_fusion.mask_ref), custom_call_target="tpu_custom_call" | custom-call | flops 7247757312 | bytes 18874368 | tf_op jit(solution)/shard_map/forward_tiles/pallas_call | solution.py:175
  290.0 5.5 all-to-all-start.9
  298.8 8.8 %all-to-all-done.9 = bf16[8,1,16,1536]{3,2,1,0:T(8,128)(2,1)} async-done(((bf16[8,1,16,1536]{3,2,1,0:T(8,128)(2,1)}), bf16[8,1,16,1536]{3,2,1,0:T(8,128)(2,1)}, u32[]{:S(2)}, u32[]{:S(2)}) %all-to-all-start.9) | async-done | bytes 393248 | tf_op jit(solution)/shard_map/all_to_all | solution.py:199
  311.1 15.7 %all_to_all.124 = bf16[8,1,16,1536]{3,2,1,0:T(8,128)(2,1)S(1)} all-to-all(bf16[8,1,16,1536]{3,2,1,0:T(8,128)(2,1)S(1)} %bitcast.503), channel_id=1, replica_groups=mesh['freq'=8,'pts'=4] {'freq'}, dimensions={0} | all-to-all | bytes 786432 | tf_op jit(solution)/shard_map/all_to_all | solution.py:190
  327.0 13.2 %adjoint_tiles.9 = bf16[4,8,16,1536]{3,2,1,0:T(8,128)(2,1)} custom-call(bf16[8,16,1536]{2,1,0:T(8,128)(2,1)S(1)} %bitcast.429, bf16[16,6,24,16,256]{4,3,2,1,0:T(8,128)(2,1)} %bitcast.439, bf16[16,6,24,16,256]{4,3,2,1,0:T(8,128)(2,1)} %bitcast.451, f32[16,24,128]{2,1,0:T(8,128)S(1)} %pad_convert_fusion.mask_ref), custom_call_target="tpu_custom_call" | custom-call | flops 7247757312 | bytes 18874368 | tf_op jit(solution)/shard_map/adjoint_tiles/pallas_call | solution.py:182
  342.8 15.0 %all_to_all.125 = bf16[8,1,16,1536]{3,2,1,0:T(8,128)(2,1)S(1)} all-to-all(bf16[8,1,16,1536]{3,2,1,0:T(8,128)(2,1)S(1)} %bitcast.504), channel_id=1, replica_groups=mesh['freq'=8,'pts'=4] {'freq'}, dimensions={0} | all-to-all | bytes 786432 | tf_op jit(solution)/shard_map/all_to_all | solution.py:190
  358.0 13.2 %adjoint_tiles.8 = bf16[4,8,16,1536]{3,2,1,0:T(8,128)(2,1)} custom-call(bf16[8,16,1536]{2,1,0:T(8,128)(2,1)S(1)} %bitcast.430, bf16[16,6,24,16,256]{4,3,2,1,0:T(8,128)(2,1)} %bitcast.440, bf16[16,6,24,16,256]{4,3,2,1,0:T(8,128)(2,1)} %bitcast.452, f32[16,24,128]{2,1,0:T(8,128)S(1)} %pad_convert_fusion.mask_ref), custom_call_target="tpu_custom_call" | custom-call | flops 7247757312 | bytes 18874368 | tf_op jit(solution)/shard_map/adjoint_tiles/pallas_call | solution.py:182
  373.3 4.1 all-to-all-start.15
  377.4 19.8 %reduce-scatter.11.cloned.1.call-done = bf16[1,8,16,1536]{3,2,1,0:T(8,128)(2,1)} async-done(((bf16[4,8,16,1536]{3,2,1,0:T(8,128)(2,1)}), bf16[1,8,16,1536]{3,2,1,0:T(8,128)(2,1)}) %reduce-scatter.11.cloned.1.call-update) | async-done | bytes 393232 | tf_op jit(solution)/shard_map/reduce_scatter | solution.py:216
  399.2 5.5 all-to-all-start.13
  408.1 8.3 %all-to-all-done.13 = bf16[8,1,16,1536]{3,2,1,0:T(8,128)(2,1)} async-done(((bf16[8,1,16,1536]{3,2,1,0:T(8,128)(2,1)}), bf16[8,1,16,1536]{3,2,1,0:T(8,128)(2,1)}, u32[]{:S(2)}, u32[]{:S(2)}) %all-to-all-start.13) | async-done | bytes 393248 | tf_op jit(solution)/shard_map/all_to_all | solution.py:199
  421.4 15.3 %all_to_all.126 = bf16[8,1,16,1536]{3,2,1,0:T(8,128)(2,1)S(1)} all-to-all(bf16[8,1,16,1536]{3,2,1,0:T(8,128)(2,1)S(1)} %bitcast.505), channel_id=1, replica_groups=mesh['freq'=8,'pts'=4] {'freq'}, dimensions={0} | all-to-all | bytes 786432 | tf_op jit(solution)/shard_map/all_to_all | solution.py:190
  440.7 14.8 %all_to_all.127 = bf16[8,1,16,1536]{3,2,1,0:T(8,128)(2,1)S(1)} all-to-all(bf16[8,1,16,1536]{3,2,1,0:T(8,128)(2,1)S(1)} %bitcast.506), channel_id=1, replica_groups=mesh['freq'=8,'pts'=4] {'freq'}, dimensions={0} | all-to-all | bytes 786432 | tf_op jit(solution)/shard_map/all_to_all | solution.py:190
  458.0 12.7 %forward_tiles.11 = bf16[8,16,1536]{2,1,0:T(8,128)(2,1)S(1)} custom-call(bf16[4,8,16,1536]{3,2,1,0:T(8,128)(2,1)S(1)} %copy-done.3, bf16[16,6,24,16,256]{4,3,2,1,0:T(8,128)(2,1)} %bitcast.441, bf16[16,6,24,16,256]{4,3,2,1,0:T(8,128)(2,1)} %bitcast.453, f32[16,6,384]{2,1,0:T(8,128)S(1)} %compare_convert_fusion.mask_ref), custom_call_target="tpu_custom_call" | custom-call | flops 7247757312 | bytes 18874368 | tf_op jit(solution)/shard_map/forward_tiles/pallas_call | solution.py:175
  471.7 4.3 all-to-all-start.19
  477.8 12.5 %forward_tiles.10 = bf16[8,16,1536]{2,1,0:T(8,128)(2,1)S(1)} custom-call(bf16[4,8,16,1536]{3,2,1,0:T(8,128)(2,1)S(1)} %copy-done.4, bf16[16,6,24,16,256]{4,3,2,1,0:T(8,128)(2,1)} %bitcast.442, bf16[16,6,24,16,256]{4,3,2,1,0:T(8,128)(2,1)} %bitcast.454, f32[16,6,384]{2,1,0:T(8,128)S(1)} %compare_convert_fusion.mask_ref), custom_call_target="tpu_custom_call" | custom-call | flops 7247757312 | bytes 18874368 | tf_op jit(solution)/shard_map/forward_tiles/pallas_call | solution.py:175
  491.4 5.6 all-to-all-start.17
  500.3 8.8 %all-to-all-done.17 = bf16[8,1,16,1536]{3,2,1,0:T(8,128)(2,1)} async-done(((bf16[8,1,16,1536]{3,2,1,0:T(8,128)(2,1)}), bf16[8,1,16,1536]{3,2,1,0:T(8,128)(2,1)}, u32[]{:S(2)}, u32[]{:S(2)}) %all-to-all-start.17) | async-done | bytes 393248 | tf_op jit(solution)/shard_map/all_to_all | solution.py:199
  509.1 5.6 add_add_fusion
  515.3 15.7 %all_to_all.128 = bf16[8,1,16,1536]{3,2,1,0:T(8,128)(2,1)S(1)} all-to-all(bf16[8,1,16,1536]{3,2,1,0:T(8,128)(2,1)S(1)} %bitcast.497), channel_id=1, replica_groups=mesh['freq'=8,'pts'=4] {'freq'}, dimensions={0} | all-to-all | bytes 786432 | tf_op jit(solution)/shard_map/all_to_all | solution.py:190
  531.3 13.2 %adjoint_tiles.11 = bf16[4,8,16,1536]{3,2,1,0:T(8,128)(2,1)} custom-call(bf16[8,16,1536]{2,1,0:T(8,128)(2,1)S(1)} %bitcast.432, bf16[16,6,24,16,256]{4,3,2,1,0:T(8,128)(2,1)} %bitcast.443, bf16[16,6,24,16,256]{4,3,2,1,0:T(8,128)(2,1)} %bitcast.455, f32[16,24,128]{2,1,0:T(8,128)S(1)} %pad_convert_fusion.mask_ref), custom_call_target="tpu_custom_call" | custom-call | flops 7247757312 | bytes 18874368 | tf_op jit(solution)/shard_map/adjoint_tiles/pallas_call | solution.py:182
  546.6 15.0 %all_to_all.129 = bf16[8,1,16,1536]{3,2,1,0:T(8,128)(2,1)S(1)} all-to-all(bf16[8,1,16,1536]{3,2,1,0:T(8,128)(2,1)S(1)} %bitcast.487), channel_id=1, replica_groups=mesh['freq'=8,'pts'=4] {'freq'}, dimensions={0} | all-to-all | bytes 786432 | tf_op jit(solution)/shard_map/all_to_all | solution.py:190
  561.8 13.2 %adjoint_tiles.10 = bf16[4,8,16,1536]{3,2,1,0:T(8,128)(2,1)} custom-call(bf16[8,16,1536]{2,1,0:T(8,128)(2,1)S(1)} %bitcast.421, bf16[16,6,24,16,256]{4,3,2,1,0:T(8,128)(2,1)} %bitcast.444, bf16[16,6,24,16,256]{4,3,2,1,0:T(8,128)(2,1)} %bitcast.456, f32[16,24,128]{2,1,0:T(8,128)S(1)} %pad_convert_fusion.mask_ref), custom_call_target="tpu_custom_call" | custom-call | flops 7247757312 | bytes 18874368 | tf_op jit(solution)/shard_map/adjoint_tiles/pallas_call | solution.py:182
  580.6 20.5 %reduce-scatter.15.cloned.1.call-done = bf16[1,8,16,1536]{3,2,1,0:T(8,128)(2,1)} async-done(((bf16[4,8,16,1536]{3,2,1,0:T(8,128)(2,1)}), bf16[1,8,16,1536]{3,2,1,0:T(8,128)(2,1)}) %reduce-scatter.15.cloned.1.call-update) | async-done | bytes 393232 | tf_op jit(solution)/shard_map/reduce_scatter | solution.py:216
  603.1 5.5 all-to-all-start.21
  610.3 3.5 copy.88
  620.3 6.1 fusion.18
  (199 shorter events, 107.7 us)
Async XLA Ops:
  9.6 21.7 %copy-start.12 = (bf16[8,1,16,512]{3,2,1,0:T(8,128)(2,1)}, bf16[8,1,16,512]{3,2,1,0:T(8,128)(2,1)S(1)}, u32[]{:S(2)}) copy-start(bf16[8,1,16,512]{3,2,1,0:T(8,128)(2,1)S(1)} %get-tuple-element.14) | copy-start | bytes 393220
  9.6 21.7 %copy-start.14 = (bf16[8,1,16,512]{3,2,1,0:T(8,128)(2,1)}, bf16[8,1,16,512]{3,2,1,0:T(8,128)(2,1)S(1)}, u32[]{:S(2)}) copy-start(bf16[8,1,16,512]{3,2,1,0:T(8,128)(2,1)S(1)} %get-tuple-element.15) | copy-start | bytes 393220
  10.8 37.1 %copy-start.38 = (s32[16,6,24]{2,0,1:T(8,128)S(1)}, s32[16,6,24]{2,0,1:T(8,128)}, u32[]{:S(2)}) copy-start(s32[16,6,24]{2,0,1:T(8,128)} %param.9) | copy-start | bytes 27652
  10.8 19.1 %all-to-all-start.2 = ((bf16[8,1,16,1536]{3,2,1,0:T(8,128)(2,1)}), bf16[8,1,16,1536]{3,2,1,0:T(8,128)(2,1)S(1)}, u32[]{:S(2)}, u32[]{:S(2)}) async-start(bf16[8,1,16,1536]{3,2,1,0:T(8,128)(2,1)} %bitcast.25), calls=%async_computation.2 | async-start | bytes 786432 | tf_op jit(solution)/shard_map/all_to_all | solution.py:190
  18.2 31.5 %all-gather.9.cloned.1.call-start = ((), (), s32[]{:S(2)}) async-start(), calls=%async_computation.31 | async-start | bytes 1966080 | tf_op jit(solution)/shard_map/all_gather | solution.py:207
  18.5 29.5 %copy-start.27 = (bf16[128,128]{1,0:T(8,128)(2,1)}, bf16[128,128]{1,0:T(8,128)(2,1)S(1)}, u32[]{:S(2)}) copy-start(bf16[128,128]{1,0:T(8,128)(2,1)S(1)} %get-tuple-element.5) | copy-start | bytes 98308
  18.5 67.1 %copy-start.21 = (bf16[128,128]{1,0:T(8,128)(2,1)}, bf16[128,128]{1,0:T(8,128)(2,1)S(1)}, u32[]{:S(2)}) copy-start(bf16[128,128]{1,0:T(8,128)(2,1)S(1)} %get-tuple-element.4) | copy-start | bytes 98308
  30.9 40.7 %all-gather.7.cloned.1.call-start = ((), (), s32[]{:S(2)}) async-start(), calls=%async_computation.30 | async-start | bytes 1966080 | tf_op jit(solution)/shard_map/all_gather | solution.py:207
  64.8 21.8 %all-to-all-start.3 = ((bf16[8,1,16,1536]{3,2,1,0:T(8,128)(2,1)}), bf16[8,1,16,1536]{3,2,1,0:T(8,128)(2,1)S(1)}, u32[]{:S(2)}, u32[]{:S(2)}) async-start(bf16[8,1,16,1536]{3,2,1,0:T(8,128)(2,1)} %bitcast.30), calls=%async_computation.3 | async-start | bytes 786432 | tf_op jit(solution)/shard_map/all_to_all | solution.py:199
  73.1 19.1 %copy-start.36 = (bf16[128,2,512]{2,0,1:T(8,128)(2,1)S(1)}, bf16[128,2,512]{2,0,1:T(8,128)(2,1)}, u32[]{:S(2)}) copy-start(bf16[128,2,512]{2,0,1:T(8,128)(2,1)} %get-tuple-element.30) | copy-start | bytes 786436
  73.1 19.5 %copy-start.40 = (s32[1,1536]{1,0:T(1,128)S(1)}, s32[1,1536]{1,0:T(1,128)}, u32[]{:S(2)}) copy-start(s32[1,1536]{1,0:T(1,128)} %param.6) | copy-start | bytes 18436
  86.7 17.7 %all-to-all-start.1 = ((bf16[8,1,16,1536]{3,2,1,0:T(8,128)(2,1)}), bf16[8,1,16,1536]{3,2,1,0:T(8,128)(2,1)}, u32[]{:S(2)}, u32[]{:S(2)}) async-start(bf16[8,1,16,1536]{3,2,1,0:T(8,128)(2,1)} %bitcast.15), calls=%async_computation.1 | async-start | bytes 786432 | tf_op jit(solution)/shard_map/all_to_all | solution.py:199
  108.5 15.6 %all-to-all-start.6 = ((bf16[8,1,16,1536]{3,2,1,0:T(8,128)(2,1)}), bf16[8,1,16,1536]{3,2,1,0:T(8,128)(2,1)}, u32[]{:S(2)}, u32[]{:S(2)}) async-start(bf16[8,1,16,1536]{3,2,1,0:T(8,128)(2,1)} %bitcast.474), calls=%async_computation.7 | async-start | bytes 786432 | tf_op jit(solution)/shard_map/all_to_all | solution.py:190
  112.6 56.4 %reduce-scatter.9.cloned.1.call-start = ((), (), s32[]{:S(2)}) async-start(), calls=%async_computation.33 | async-start | bytes 1966080 | tf_op jit(solution)/shard_map/reduce_scatter | solution.py:216
  138.5 57.3 %reduce-scatter.7.cloned.1.call-start = ((), (), s32[]{:S(2)}) async-start(), calls=%async_computation.32 | async-start | bytes 1966080 | tf_op jit(solution)/shard_map/reduce_scatter | solution.py:216
  138.6 16.9 %copy-start.28 = (bf16[128,128]{1,0:T(8,128)(2,1)S(1)}, bf16[128,128]{1,0:T(8,128)(2,1)}, u32[]{:S(2)}) copy-start(bf16[128,128]{1,0:T(8,128)(2,1)} %copy-done.27) | copy-start | bytes 98308
  171.0 26.8 %all-to-all-start.7 = ((bf16[8,1,16,1536]{3,2,1,0:T(8,128)(2,1)}), bf16[8,1,16,1536]{3,2,1,0:T(8,128)(2,1)}, u32[]{:S(2)}, u32[]{:S(2)}) async-start(bf16[8,1,16,1536]{3,2,1,0:T(8,128)(2,1)} %bitcast.485), calls=%async_computation.9 | async-start | bytes 786432 | tf_op jit(solution)/shard_map/all_to_all | solution.py:199
  197.8 17.2 %all-to-all-start.5 = ((bf16[8,1,16,1536]{3,2,1,0:T(8,128)(2,1)}), bf16[8,1,16,1536]{3,2,1,0:T(8,128)(2,1)}, u32[]{:S(2)}, u32[]{:S(2)}) async-start(bf16[8,1,16,1536]{3,2,1,0:T(8,128)(2,1)} %bitcast.479), calls=%async_computation.6 | async-start | bytes 786432 | tf_op jit(solution)/shard_map/all_to_all | solution.py:199
  203.4 51.5 %all-gather.13.cloned.1.call-start = ((), (), s32[]{:S(2)}) async-start(), calls=%async_computation.35 | async-start | bytes 1966080 | tf_op jit(solution)/shard_map/all_gather | solution.py:207
  219.4 16.0 %copy-start.29 = (bf16[128,128]{1,0:T(8,128)(2,1)S(1)}, bf16[128,128]{1,0:T(8,128)(2,1)}, u32[]{:S(2)}) copy-start(bf16[128,128]{1,0:T(8,128)(2,1)} %copy-done.27) | copy-start | bytes 98308
  236.4 38.6 %all-gather.11.cloned.1.call-start = ((), (), s32[]{:S(2)}) async-start(), calls=%async_computation.34 | async-start | bytes 1966080 | tf_op jit(solution)/shard_map/all_gather | solution.py:207
  236.5 17.4 %copy-start.30 = (bf16[128,128]{1,0:T(8,128)(2,1)S(1)}, bf16[128,128]{1,0:T(8,128)(2,1)}, u32[]{:S(2)}) copy-start(bf16[128,128]{1,0:T(8,128)(2,1)} %copy-done.27) | copy-start | bytes 98308
  270.0 20.0 %all-to-all-start.11 = ((bf16[8,1,16,1536]{3,2,1,0:T(8,128)(2,1)}), bf16[8,1,16,1536]{3,2,1,0:T(8,128)(2,1)}, u32[]{:S(2)}, u32[]{:S(2)}) async-start(bf16[8,1,16,1536]{3,2,1,0:T(8,128)(2,1)} %bitcast.484), calls=%async_computation.13 | async-start | bytes 786432 | tf_op jit(solution)/shard_map/all_to_all | solution.py:199
  290.0 17.7 %all-to-all-start.9 = ((bf16[8,1,16,1536]{3,2,1,0:T(8,128)(2,1)}), bf16[8,1,16,1536]{3,2,1,0:T(8,128)(2,1)}, u32[]{:S(2)}, u32[]{:S(2)}) async-start(bf16[8,1,16,1536]{3,2,1,0:T(8,128)(2,1)} %bitcast.480), calls=%async_computation.11 | async-start | bytes 786432 | tf_op jit(solution)/shard_map/all_to_all | solution.py:199
  295.5 75.8 %reduce-scatter.13.cloned.1.call-start = ((), (), s32[]{:S(2)}) async-start(), calls=%async_computation.37 | async-start | bytes 1966080 | tf_op jit(solution)/shard_map/reduce_scatter | solution.py:216
  310.4 16.4 %copy-start.11 = (f32[1,512,1536]{1,2,0:T(8,128)}, f32[1,512,1536]{1,2,0:T(8,128)S(1)}, u32[]{:S(2)}) copy-start(f32[1,512,1536]{1,2,0:T(8,128)S(1)} %fusion.8) | copy-start | bytes 9437188
  310.4 16.3 %copy-start.31 = (bf16[128,128]{1,0:T(8,128)(2,1)S(1)}, bf16[128,128]{1,0:T(8,128)(2,1)}, u32[]{:S(2)}) copy-start(bf16[128,128]{1,0:T(8,128)(2,1)} %copy-done.27) | copy-start | bytes 98308
  340.2 57.0 %reduce-scatter.11.cloned.1.call-start = ((), (), s32[]{:S(2)}) async-start(), calls=%async_computation.36 | async-start | bytes 1966080 | tf_op jit(solution)/shard_map/reduce_scatter | solution.py:216
  340.2 17.6 %copy-start.32 = (bf16[128,128]{1,0:T(8,128)(2,1)S(1)}, bf16[128,128]{1,0:T(8,128)(2,1)}, u32[]{:S(2)}) copy-start(bf16[128,128]{1,0:T(8,128)(2,1)} %copy-done.27) | copy-start | bytes 98308
  373.3 25.9 %all-to-all-start.15 = ((bf16[8,1,16,1536]{3,2,1,0:T(8,128)(2,1)}), bf16[8,1,16,1536]{3,2,1,0:T(8,128)(2,1)}, u32[]{:S(2)}, u32[]{:S(2)}) async-start(bf16[8,1,16,1536]{3,2,1,0:T(8,128)(2,1)} %bitcast.486), calls=%async_computation.19 | async-start | bytes 786432 | tf_op jit(solution)/shard_map/all_to_all | solution.py:199
  399.2 17.2 %all-to-all-start.13 = ((bf16[8,1,16,1536]{3,2,1,0:T(8,128)(2,1)}), bf16[8,1,16,1536]{3,2,1,0:T(8,128)(2,1)}, u32[]{:S(2)}, u32[]{:S(2)}) async-start(bf16[8,1,16,1536]{3,2,1,0:T(8,128)(2,1)} %bitcast.481), calls=%async_computation.16 | async-start | bytes 786432 | tf_op jit(solution)/shard_map/all_to_all | solution.py:199
  404.7 51.8 %all-gather.17.cloned.1.call-start = ((), (), s32[]{:S(2)}) async-start(), calls=%async_computation.39 | async-start | bytes 1966080 | tf_op jit(solution)/shard_map/all_gather | solution.py:207
  420.8 16.0 %copy-start.33 = (bf16[128,128]{1,0:T(8,128)(2,1)S(1)}, bf16[128,128]{1,0:T(8,128)(2,1)}, u32[]{:S(2)}) copy-start(bf16[128,128]{1,0:T(8,128)(2,1)} %copy-done.27) | copy-start | bytes 98308
  437.8 38.6 %all-gather.15.cloned.1.call-start = ((), (), s32[]{:S(2)}) async-start(), calls=%async_computation.38 | async-start | bytes 1966080 | tf_op jit(solution)/shard_map/all_gather | solution.py:207
  438.1 17.4 %copy-start.34 = (bf16[128,128]{1,0:T(8,128)(2,1)S(1)}, bf16[128,128]{1,0:T(8,128)(2,1)}, u32[]{:S(2)}) copy-start(bf16[128,128]{1,0:T(8,128)(2,1)} %copy-done.27) | copy-start | bytes 98308
  458.0 12.7 %copy-start.24 = (bf16[128,128]{1,0:T(8,128)(2,1)S(1)}, bf16[128,128]{1,0:T(8,128)(2,1)}, u32[]{:S(2)}) copy-start(bf16[128,128]{1,0:T(8,128)(2,1)} %copy-done.21) | copy-start | bytes 98308
  471.7 19.7 %all-to-all-start.19 = ((bf16[8,1,16,1536]{3,2,1,0:T(8,128)(2,1)}), bf16[8,1,16,1536]{3,2,1,0:T(8,128)(2,1)}, u32[]{:S(2)}, u32[]{:S(2)}) async-start(bf16[8,1,16,1536]{3,2,1,0:T(8,128)(2,1)} %bitcast.482), calls=%async_computation.23 | async-start | bytes 786432 | tf_op jit(solution)/shard_map/all_to_all | solution.py:199
  491.4 17.7 %all-to-all-start.17 = ((bf16[8,1,16,1536]{3,2,1,0:T(8,128)(2,1)}), bf16[8,1,16,1536]{3,2,1,0:T(8,128)(2,1)}, u32[]{:S(2)}, u32[]{:S(2)}) async-start(bf16[8,1,16,1536]{3,2,1,0:T(8,128)(2,1)} %bitcast.483), calls=%async_computation.21 | async-start | bytes 786432 | tf_op jit(solution)/shard_map/all_to_all | solution.py:199
  497.0 78.1 %reduce-scatter.17.cloned.1.call-start = ((), (), s32[]{:S(2)}) async-start(), calls=%async_computation.41 | async-start | bytes 1966080 | tf_op jit(solution)/shard_map/reduce_scatter | solution.py:216
  500.3 14.4 %copy-start.19 = (bf16[8,1,16,512]{3,2,1,0:T(8,128)(2,1)S(1)}, bf16[8,1,16,512]{3,2,1,0:T(8,128)(2,1)}, u32[]{:S(2)}) copy-start(bf16[8,1,16,512]{3,2,1,0:T(8,128)(2,1)} %copy-done.14) | copy-start | bytes 393220
  500.3 30.7 %copy-start.35 = (bf16[128,128]{1,0:T(8,128)(2,1)S(1)}, bf16[128,128]{1,0:T(8,128)(2,1)}, u32[]{:S(2)}) copy-start(bf16[128,128]{1,0:T(8,128)(2,1)} %copy-done.27) | copy-start | bytes 98308
  514.7 16.6 %copy-start.20 = (bf16[1,512,1536]{1,2,0:T(8,128)(2,1)}, bf16[1,512,1536]{1,2,0:T(8,128)(2,1)S(1)}, u32[]{:S(2)}) copy-start(bf16[1,512,1536]{1,2,0:T(8,128)(2,1)S(1)} %get-tuple-element.23) | copy-start | bytes 4718596
  531.3 13.3 %copy-start.13 = (bf16[8,1,16,512]{3,2,1,0:T(8,128)(2,1)S(1)}, bf16[8,1,16,512]{3,2,1,0:T(8,128)(2,1)}, u32[]{:S(2)}) copy-start(bf16[8,1,16,512]{3,2,1,0:T(8,128)(2,1)} %copy-done.12) | copy-start | bytes 393220
  544.5 56.6 %reduce-scatter.15.cloned.1.call-start = ((), (), s32[]{:S(2)}) async-start(), calls=%async_computation.40 | async-start | bytes 1966080 | tf_op jit(solution)/shard_map/reduce_scatter | solution.py:216
  561.8 13.2 %copy-start.26 = (bf16[128,128]{1,0:T(8,128)(2,1)S(1)}, bf16[128,128]{1,0:T(8,128)(2,1)}, u32[]{:S(2)}) copy-start(bf16[128,128]{1,0:T(8,128)(2,1)} %copy-done.21) | copy-start | bytes 98308
  575.0 33.7 %copy-start.7 = (bf16[1,512,1536]{2,1,0:T(8,128)(2,1)S(1)}, bf16[1,512,1536]{2,1,0:T(8,128)(2,1)}, u32[]{:S(2)}) copy-start(bf16[1,512,1536]{2,1,0:T(8,128)(2,1)} %param.5) | copy-start | bytes 4718596
  577.2 26.0 %all-to-all-start.23 = ((bf16[8,1,16,1536]{3,2,1,0:T(8,128)(2,1)}), bf16[8,1,16,1536]{3,2,1,0:T(8,128)(2,1)S(1)}, u32[]{:S(2)}, u32[]{:S(2)}) async-start(bf16[8,1,16,1536]{3,2,1,0:T(8,128)(2,1)} %bitcast.158), calls=%async_computation.29 | async-start | bytes 786432 | tf_op jit(solution)/shard_map/all_to_all | solution.py:199
  603.1 17.2 %all-to-all-start.21 = ((bf16[8,1,16,1536]{3,2,1,0:T(8,128)(2,1)}), bf16[8,1,16,1536]{3,2,1,0:T(8,128)(2,1)}, u32[]{:S(2)}, u32[]{:S(2)}) async-start(bf16[8,1,16,1536]{3,2,1,0:T(8,128)(2,1)} %bitcast.147), calls=%async_computation.26 | async-start | bytes 786432 | tf_op jit(solution)/shard_map/all_to_all | solution.py:199
  (19 other events, 90.1 us)
Sparse Core Ops, SparseCore 0:
  31.1 18.6 all-gather.8
  51.9 19.7 all-gather.6
  138.7 26.1 reduce-scatter.8
  169.1 26.6 reduce-scatter.6
  236.5 17.3 all-gather.12
  255.3 19.6 all-gather.10
  340.3 25.7 reduce-scatter.12
  371.4 25.7 reduce-scatter.10
  437.9 17.3 all-gather.16
  456.8 19.5 all-gather.14
  544.6 25.8 reduce-scatter.16
  575.2 25.9 reduce-scatter.14
